TPU v7x, 512 devices: a whole 4x4x16 slice. The times are simulated.
512 devices in a mesh: section: 4 (over z_lo), th: 16 (over z_hi, y), tw: 8 (over x, core).
Axes of the slice: x: 4, y: 4, z: 16 (z_hi: 4, z_lo: 4; z = z_hi * 4 + z_lo), core: 2. Of those that a mesh axis runs over, the one named last changes fastest.
Arguments:
- features: bfloat16 [16, 256, 256, 128], P('section', 'th', 'tw'), may hold values from -11 to 11, as said below
- norm_gain: float32 [128], replicated, may hold values from 0.25 to 1.75
- norm_shift: float32 [128], replicated, may hold values from -3 to 3
- first_kernel: bfloat16 [3, 3, 3, 128, 128], replicated, may hold values from -0.109375 to 0.109375
- second_gain: float32 [128], replicated, may hold values from 0.25 to 1.75
- second_shift: float32 [128], replicated, may hold values from -3 to 3
- second_kernel: bfloat16 [3, 3, 3, 128, 128], replicated, may hold values from -0.109375 to 0.109375
Outputs:
- block_out: bfloat16 [16, 256, 256, 128], P('section', 'th', 'tw')
Inputs may be any that keep to these rules, and one draw needn't show every extreme that they name: `features`: activations of order one.
All inputs are finite; a program needn't handle non-finite values.
Results may differ from a plain program's by a relative error of at most 0.0038.
Values may be sent and summed in bfloat16 or wider, within the bound.
No kernel may reach another device: no remote copies, remote signals or barrier semaphores. Data moves between devices by JAX's collectives and lax.ppermute only.
A program may use at most 128 MiB of HBM per device.

v0:
```python
import jax
import jax.numpy as jnp
from jax import lax
from jax.sharding import Mesh
from jax.sharding import PartitionSpec as P

GROUPS = 32
TH = ("th_0", "th_1")
TW = ("tw_0", "tw_1")
SECTION_TH_TW = ("section", "th_0", "th_1", "tw_0", "tw_1")


def by_axis(value, axes):
    for axis in axes:
        value = lax.psum(value, axis)
    return value


def passed_along(value, axis, steps):
    count = lax.axis_size(axis)
    initial, last = (max(0, -steps), min(count, count - steps))
    return lax.ppermute(value, axis, [(source, source + steps) for source in range(initial, last)])


def extended(cells, sides, width):
    for axis, dim in sides:
        count = lax.axis_size(axis)
        ends = count - 1
        head = lax.slice_in_dim(cells, 0, width, axis=dim)
        tail = lax.slice_in_dim(cells, cells.shape[dim] - width, cells.shape[dim], axis=dim)
        cells = jnp.concatenate(
            [
                lax.ppermute(tail, axis, [(i, (i + 1) % count) for i in range(ends)]),
                cells,
                lax.ppermute(head, axis, [((i + 1) % count, i) for i in range(ends)]),
            ],
            axis=dim,
        )
    return cells


def causal_conv(padded, kernel):
    frames = padded.shape[0] - 2
    rows = padded.shape[1] - 2
    cols = padded.shape[2] - 2
    chans = padded.shape[3]
    stacked = jnp.concatenate([padded[:, :, d : d + cols, :] for d in range(3)], axis=-1)
    taps = kernel.reshape(3, 3, 3 * chans, kernel.shape[-1])
    total = jnp.zeros((frames * rows * cols, kernel.shape[-1]), jnp.float32)
    for dt in range(3):
        for dh in range(3):
            window = stacked[dt : dt + frames, dh : dh + rows].reshape(-1, 3 * chans)
            total = total + jnp.dot(window, taps[dt, dh], preferred_element_type=jnp.float32)
    return total.reshape(frames, rows, cols, kernel.shape[-1])


def group_totals(values):
    chans = values.shape[-1]
    return jnp.sum(values.reshape(-1, GROUPS, chans // GROUPS), axis=(0, 2))


def group_moments(interior):
    chans = interior.shape[-1]
    count = (
        interior.size // GROUPS * lax.axis_size("section") * lax.axis_size(TH) * lax.axis_size(TW)
    )
    first, second = (
        by_axis(group_totals(interior), SECTION_TH_TW),
        by_axis(group_totals(interior * interior), SECTION_TH_TW),
    )
    mean = first / count
    var = second / count - mean * mean
    return (jnp.repeat(mean, chans // GROUPS), jnp.repeat(var, chans // GROUPS))


def normalize_act(values, moments, gain, shift):
    mean, var = moments
    normed = (values - mean) / jnp.sqrt(var + 1e-06) * gain + shift
    return jax.nn.silu(normed).astype(jnp.bfloat16)


def extend_each(act):
    earlier = passed_along(act[-2:], "section", 1)
    longer = jnp.concatenate([earlier, act], axis=0)
    return extended(longer, ((TH, 1), (TW, 2)), 1)


def shards(features, norm_gain, norm_shift, first_kernel, second_gain, second_shift, second_kernel):
    inputs = features.astype(jnp.float32)
    first_act = normalize_act(inputs, group_moments(inputs), norm_gain, norm_shift)
    hidden = causal_conv(extend_each(first_act), first_kernel)
    second_act = normalize_act(hidden, group_moments(hidden), second_gain, second_shift)
    second_padded = extend_each(second_act)
    branch = causal_conv(second_padded, second_kernel)
    return (inputs + branch).astype(jnp.bfloat16)


def solution(mesh):
    torus = Mesh(
        mesh.devices.reshape(mesh.shape["section"], 4, 4, 4, 2),
        ("section", "th_0", "th_1", "tw_0", "tw_1"),
    )
    return jax.shard_map(
        shards,
        mesh=torus,
        in_specs=(P("section", TH, TW, None), P(), P(), P(), P(), P(), P()),
        out_specs=P("section", TH, TW, None),
        check_vma=False,
    )
```

profile of v0, /device:TPU:25, one launch (start us, length us, event | category | flops | bytes accessed | tf_op | source)
XLA Modules:
  0.0 200.5 jit_solution(3000817920652636523)
XLA Ops:
  0.0 1.3 convert_reduce_fusion
  1.8 11.0 %all-reduce.7 = (f32[32]{0:T(128)S(1)}, f32[32]{0:T(128)S(1)}) all-reduce(f32[32]{0:T(128)S(1)} %reduce_sum.54, f32[32]{0:T(128)S(1)} %reduce_sum.51), channel_id=1, replica_groups=mesh['section'=4,'th_0'=4,'th_1'=4,'tw_0'=4,'tw_1'=2] {'section'}, use_global_device_ids=true, to_apply=%region_9.0 | all-reduce | flops 64 | bytes 512 | tf_op jit(solution)/shard_map/psum | solution.py:15
  12.7 16.9 %all-reduce.5 = (f32[32]{0:T(128)S(1)}, f32[32]{0:T(128)S(1)}) all-reduce(f32[32]{0:T(128)S(1)} %get-tuple-element.23, f32[32]{0:T(128)S(1)} %get-tuple-element.24), channel_id=1, replica_groups=mesh['section'=4,'th_0'=4,'th_1'=4,'tw_0'=4,'tw_1'=2] {'th_0'}, use_global_device_ids=true, to_apply=%region_10.0 | all-reduce | flops 64 | bytes 512 | tf_op jit(solution)/shard_map/psum | solution.py:15
  29.6 5.7 %all-reduce.3 = (f32[32]{0:T(128)S(1)}, f32[32]{0:T(128)S(1)}) all-reduce(f32[32]{0:T(128)S(1)} %get-tuple-element.19, f32[32]{0:T(128)S(1)} %get-tuple-element.20), channel_id=1, replica_groups=mesh['section'=4,'th_0'=4,'th_1'=4,'tw_0'=4,'tw_1'=2] {'th_1'}, use_global_device_ids=true, to_apply=%region_11.0 | all-reduce | flops 64 | bytes 512 | tf_op jit(solution)/shard_map/psum | solution.py:15
  35.3 8.4 %all-reduce.1 = (f32[32]{0:T(128)S(1)}, f32[32]{0:T(128)S(1)}) all-reduce(f32[32]{0:T(128)S(1)} %get-tuple-element.15, f32[32]{0:T(128)S(1)} %get-tuple-element.16), channel_id=1, replica_groups=mesh['section'=4,'th_0'=4,'th_1'=4,'tw_0'=4,'tw_1'=2] {'tw_0'}, use_global_device_ids=true, to_apply=%region_12.13 | all-reduce | flops 64 | bytes 512 | tf_op jit(solution)/shard_map/psum | solution.py:15
  43.8 10.2 %all-reduce.9 = (f32[32]{0:T(128)S(1)}, f32[32]{0:T(128)S(1)}) all-reduce(f32[32]{0:T(128)S(1)} %get-tuple-element.11, f32[32]{0:T(128)S(1)} %get-tuple-element.12), channel_id=1, replica_groups=mesh['section'=4,'th_0'=4,'th_1'=4,'tw_0'=4,'tw_1'=2] {'tw_1'}, use_global_device_ids=true, to_apply=%region_13.14 | all-reduce | flops 64 | bytes 512 | tf_op jit(solution)/shard_map/psum | solution.py:15
  54.4 1.4 multiply_convert_fusion.1
  55.9 1.7 collective-permute-start
  57.6 5.3 %collective-permute-done = bf16[2,16,32,128]{3,2,1,0:T(8,128)(2,1)S(1)} collective-permute-done((bf16[2,16,32,128]{3,2,1,0:T(8,128)(2,1)S(1)}, bf16[2,16,32,128]{3,2,1,0:T(8,128)(2,1)S(1)}, u32[]{:S(2)}, u32[]{:S(2)}) %collective-permute-start) | collective-permute-done | bytes 262176 | tf_op jit(solution)/shard_map/ppermute | solution.py:22
  62.9 8.1 %collective-permute-start.1 = (bf16[6,1,32,128]{3,2,1,0:T(8,128)(2,1)S(1)}, bf16[6,1,32,128]{3,2,1,0:T(8,128)(2,1)S(1)}, u32[]{:S(2)}, u32[]{:S(2)}) collective-permute-start(bf16[6,1,32,128]{3,2,1,0:T(8,128)(2,1)S(1)} %get-tuple-element.53), channel_id=1, source_target_pairs={{0,8},{8,16},{16,24},{24,32},{32,40},{40,48},{48,56},{56,64},{64,7... | collective-permute-start | bytes 147464 | tf_op jit(solution)/shard_map/ppermute | solution.py:33
  71.0 1.9 collective-permute-start.2
  72.9 8.9 %collective-permute-done.2 = bf16[6,1,32,128]{3,2,1,0:T(8,128)(2,1)S(1)} collective-permute-done((bf16[6,1,32,128]{3,2,1,0:T(8,128)(2,1)S(1)}, bf16[6,1,32,128]{3,2,1,0:T(8,128)(2,1)S(1)}, u32[]{:S(2)}, u32[]{:S(2)}) %collective-permute-start.2) | collective-permute-done | bytes 49184 | tf_op jit(solution)/shard_map/ppermute | solution.py:35
  81.9 3.9 %collective-permute-start.3 = (bf16[6,18,1,128]{3,2,1,0:T(2,128)(2,1)S(1)}, bf16[6,18,1,128]{3,2,1,0:T(2,128)(2,1)S(1)}, u32[]{:S(2)}, u32[]{:S(2)}) collective-permute-start(bf16[6,18,1,128]{3,2,1,0:T(2,128)(2,1)S(1)} %get-tuple-element.49), channel_id=1, source_target_pairs={{0,1},{1,2},{2,3},{3,4},{4,5},{5,6},{6,7},{8,9},{9,10},{10,11},{11... | collective-permute-start | bytes 82952 | tf_op jit(solution)/shard_map/ppermute | solution.py:33
  85.8 2.1 %collective-permute-start.4 = (bf16[6,18,1,128]{3,2,1,0:T(2,128)(2,1)S(1)}, bf16[6,18,1,128]{3,2,1,0:T(2,128)(2,1)S(1)}, u32[]{:S(2)}, u32[]{:S(2)}) collective-permute-start(bf16[6,18,1,128]{3,2,1,0:T(2,128)(2,1)S(1)} %get-tuple-element.50), channel_id=1, source_target_pairs={{1,0},{2,1},{3,2},{4,3},{5,4},{6,5},{7,6},{9,8},{10,9},{11,10},{12... | collective-permute-start | bytes 82952 | tf_op jit(solution)/shard_map/ppermute | solution.py:35
  87.9 3.4 %collective-permute-done.4 = bf16[6,18,1,128]{3,2,1,0:T(2,128)(2,1)S(1)} collective-permute-done((bf16[6,18,1,128]{3,2,1,0:T(2,128)(2,1)S(1)}, bf16[6,18,1,128]{3,2,1,0:T(2,128)(2,1)S(1)}, u32[]{:S(2)}, u32[]{:S(2)}) %collective-permute-start.4) | collective-permute-done | bytes 27680 | tf_op jit(solution)/shard_map/ppermute | solution.py:35
  91.3 4.5 %fusion.2 = bf16[6,18,32,384]{3,2,1,0:T(8,128)(2,1)S(1)} fusion(bf16[6,18,1,128]{3,2,1,0:T(2,128)(2,1)S(1)} %collective-permute-done.4, bf16[6,1,32,128]{3,2,1,0:T(8,128)(2,1)S(1)} %collective-permute-done.2, bf16[6,1,32,128]{3,2,1,0:T(8,128)(2,1)S(1)} %collective-permute-done.1, bf16[4,16,32,128]{3,2,1,0:T(8,128)(2,1)S(1)} %multiply_convert_fusion.1, ...), kind=kLoop, calls=%fused_computation.11 | loop fusion | flops 37158912 | bytes 3594240 | tf_op jit(solution)/shard_map/concatenate | solution.py:47
  95.8 2.2 %fusion.41 = (bf16[4,16,32,384]{3,2,1,0:T(8,128)(2,1)S(1)}, bf16[4,16,32,384]{3,2,1,0:T(8,128)(2,1)S(1)}, bf16[4,16,32,384]{3,2,1,0:T(8,128)(2,1)S(1)}, bf16[4,1...) fusion(bf16[6,18,32,384]{3,2,1,0:T(8,128)(2,1)S(1)} %fusion.2), kind=kLoop, calls=%fused_computation.100 | loop fusion | bytes 28311552 | tf_op jit(solution)/shard_map/slice | solution.py:52
  103.9 10.5 %all-reduce.6 = (f32[32]{0:T(128)S(1)}, f32[32]{0:T(128)S(1)}) all-reduce(f32[32]{0:T(128)S(1)} %reduce_sum.75, f32[32]{0:T(128)S(1)} %reduce_sum.72), channel_id=1, replica_groups=mesh['section'=4,'th_0'=4,'th_1'=4,'tw_0'=4,'tw_1'=2] {'section'}, use_global_device_ids=true, to_apply=%region_23.24 | all-reduce | flops 64 | bytes 512 | tf_op jit(solution)/shard_map/psum | solution.py:15
  114.5 10.3 %all-reduce.4 = (f32[32]{0:T(128)S(1)}, f32[32]{0:T(128)S(1)}) all-reduce(f32[32]{0:T(128)S(1)} %get-tuple-element.21, f32[32]{0:T(128)S(1)} %get-tuple-element.22), channel_id=1, replica_groups=mesh['section'=4,'th_0'=4,'th_1'=4,'tw_0'=4,'tw_1'=2] {'th_0'}, use_global_device_ids=true, to_apply=%region_24.25 | all-reduce | flops 64 | bytes 512 | tf_op jit(solution)/shard_map/psum | solution.py:15
  124.8 5.7 %all-reduce.2 = (f32[32]{0:T(128)S(1)}, f32[32]{0:T(128)S(1)}) all-reduce(f32[32]{0:T(128)S(1)} %get-tuple-element.17, f32[32]{0:T(128)S(1)} %get-tuple-element.18), channel_id=1, replica_groups=mesh['section'=4,'th_0'=4,'th_1'=4,'tw_0'=4,'tw_1'=2] {'th_1'}, use_global_device_ids=true, to_apply=%region_25.26 | all-reduce | flops 64 | bytes 512 | tf_op jit(solution)/shard_map/psum | solution.py:15
  130.5 6.8 %all-reduce = (f32[32]{0:T(128)S(1)}, f32[32]{0:T(128)S(1)}) all-reduce(f32[32]{0:T(128)S(1)} %get-tuple-element.13, f32[32]{0:T(128)S(1)} %get-tuple-element.14), channel_id=1, replica_groups=mesh['section'=4,'th_0'=4,'th_1'=4,'tw_0'=4,'tw_1'=2] {'tw_0'}, use_global_device_ids=true, to_apply=%region_26.27 | all-reduce | flops 64 | bytes 512 | tf_op jit(solution)/shard_map/psum | solution.py:15
  137.3 9.1 %all-reduce.8 = (f32[32]{0:T(128)S(1)}, f32[32]{0:T(128)S(1)}) all-reduce(f32[32]{0:T(128)S(1)} %get-tuple-element.9, f32[32]{0:T(128)S(1)} %get-tuple-element.10), channel_id=1, replica_groups=mesh['section'=4,'th_0'=4,'th_1'=4,'tw_0'=4,'tw_1'=2] {'tw_1'}, use_global_device_ids=true, to_apply=%region_27.28 | all-reduce | flops 64 | bytes 512 | tf_op jit(solution)/shard_map/psum | solution.py:15
  147.2 1.3 collective-permute-start.5
  148.5 5.6 %collective-permute-done.5 = bf16[2,16,32,128]{3,2,1,0:T(8,128)(2,1)S(1)} collective-permute-done((bf16[2,16,32,128]{3,2,1,0:T(8,128)(2,1)S(1)}, bf16[2,16,32,128]{3,2,1,0:T(8,128)(2,1)S(1)}, u32[]{:S(2)}, u32[]{:S(2)}) %collective-permute-start.5) | collective-permute-done | bytes 262176 | tf_op jit(solution)/shard_map/ppermute | solution.py:22
  154.1 9.5 %collective-permute-start.6 = (bf16[6,1,32,128]{3,2,1,0:T(8,128)(2,1)S(1)}, bf16[6,1,32,128]{3,2,1,0:T(8,128)(2,1)S(1)}, u32[]{:S(2)}, u32[]{:S(2)}) collective-permute-start(bf16[6,1,32,128]{3,2,1,0:T(8,128)(2,1)S(1)} %get-tuple-element.51), channel_id=1, source_target_pairs={{0,8},{8,16},{16,24},{24,32},{32,40},{40,48},{48,56},{56,64},{64,7... | collective-permute-start | bytes 147464 | tf_op jit(solution)/shard_map/ppermute | solution.py:33
  163.6 1.9 collective-permute-start.7
  165.5 8.9 %collective-permute-done.7 = bf16[6,1,32,128]{3,2,1,0:T(8,128)(2,1)S(1)} collective-permute-done((bf16[6,1,32,128]{3,2,1,0:T(8,128)(2,1)S(1)}, bf16[6,1,32,128]{3,2,1,0:T(8,128)(2,1)S(1)}, u32[]{:S(2)}, u32[]{:S(2)}) %collective-permute-start.7) | collective-permute-done | bytes 49184 | tf_op jit(solution)/shard_map/ppermute | solution.py:35
  174.5 7.1 %collective-permute-start.8 = (bf16[6,18,1,128]{3,2,1,0:T(2,128)(2,1)S(1)}, bf16[6,18,1,128]{3,2,1,0:T(2,128)(2,1)S(1)}, u32[]{:S(2)}, u32[]{:S(2)}) collective-permute-start(bf16[6,18,1,128]{3,2,1,0:T(2,128)(2,1)S(1)} %get-tuple-element.47), channel_id=1, source_target_pairs={{0,1},{1,2},{2,3},{3,4},{4,5},{5,6},{6,7},{8,9},{9,10},{10,11},{11... | collective-permute-start | bytes 82952 | tf_op jit(solution)/shard_map/ppermute | solution.py:33
  181.7 2.1 %collective-permute-start.9 = (bf16[6,18,1,128]{3,2,1,0:T(2,128)(2,1)S(1)}, bf16[6,18,1,128]{3,2,1,0:T(2,128)(2,1)S(1)}, u32[]{:S(2)}, u32[]{:S(2)}) collective-permute-start(bf16[6,18,1,128]{3,2,1,0:T(2,128)(2,1)S(1)} %get-tuple-element.48), channel_id=1, source_target_pairs={{1,0},{2,1},{3,2},{4,3},{5,4},{6,5},{7,6},{9,8},{10,9},{11,10},{12... | collective-permute-start | bytes 82952 | tf_op jit(solution)/shard_map/ppermute | solution.py:35
  183.8 3.4 %collective-permute-done.9 = bf16[6,18,1,128]{3,2,1,0:T(2,128)(2,1)S(1)} collective-permute-done((bf16[6,18,1,128]{3,2,1,0:T(2,128)(2,1)S(1)}, bf16[6,18,1,128]{3,2,1,0:T(2,128)(2,1)S(1)}, u32[]{:S(2)}, u32[]{:S(2)}) %collective-permute-start.9) | collective-permute-done | bytes 27680 | tf_op jit(solution)/shard_map/ppermute | solution.py:35
  187.1 4.5 %fusion = bf16[6,18,32,384]{3,2,1,0:T(8,128)(2,1)S(1)} fusion(bf16[6,18,1,128]{3,2,1,0:T(2,128)(2,1)S(1)} %collective-permute-done.9, bf16[6,1,32,128]{3,2,1,0:T(8,128)(2,1)S(1)} %collective-permute-done.7, bf16[6,1,32,128]{3,2,1,0:T(8,128)(2,1)S(1)} %collective-permute-done.6, bf16[4,16,32,128]{3,2,1,0:T(8,128)(2,1)S(1)} %multiply_convert_fusion, ...), kind=kLoop, calls=%fused_computation.1 | loop fusion | flops 37158912 | bytes 3594240 | tf_op jit(solution)/shard_map/concatenate | solution.py:47
  191.6 2.2 %fusion.40 = (bf16[4,16,32,384]{3,2,1,0:T(8,128)(2,1)S(1)}, bf16[4,16,32,384]{3,2,1,0:T(8,128)(2,1)S(1)}, bf16[4,16,32,384]{3,2,1,0:T(8,128)(2,1)S(1)}, bf16[4,1...) fusion(bf16[6,18,32,384]{3,2,1,0:T(8,128)(2,1)S(1)} %fusion), kind=kLoop, calls=%fused_computation.99 | loop fusion | bytes 28311552 | tf_op jit(solution)/shard_map/slice | solution.py:52
  (58 shorter events, 14.1 us)
Async XLA Ops:
  55.9 7.0 %collective-permute-start = (bf16[2,16,32,128]{3,2,1,0:T(8,128)(2,1)S(1)}, bf16[2,16,32,128]{3,2,1,0:T(8,128)(2,1)S(1)}, u32[]{:S(2)}, u32[]{:S(2)}) collective-permute-start(bf16[2,16,32,128]{3,2,1,0:T(8,128)(2,1)S(1)} %slice.204), channel_id=1, source_target_pairs={{0,128},{128,256},{256,384},{1,129},{129,257},{257,385},{2,130},{1... | collective-permute-start | bytes 786440 | tf_op jit(solution)/shard_map/ppermute | solution.py:22
  62.9 10.1 %collective-permute-start.1 = (bf16[6,1,32,128]{3,2,1,0:T(8,128)(2,1)S(1)}, bf16[6,1,32,128]{3,2,1,0:T(8,128)(2,1)S(1)}, u32[]{:S(2)}, u32[]{:S(2)}) collective-permute-start(bf16[6,1,32,128]{3,2,1,0:T(8,128)(2,1)S(1)} %get-tuple-element.53), channel_id=1, source_target_pairs={{0,8},{8,16},{16,24},{24,32},{32,40},{40,48},{48,56},{56,64},{64,7... | collective-permute-start | bytes 147464 | tf_op jit(solution)/shard_map/ppermute | solution.py:33
  71.0 10.9 %collective-permute-start.2 = (bf16[6,1,32,128]{3,2,1,0:T(8,128)(2,1)S(1)}, bf16[6,1,32,128]{3,2,1,0:T(8,128)(2,1)S(1)}, u32[]{:S(2)}, u32[]{:S(2)}) collective-permute-start(bf16[6,1,32,128]{3,2,1,0:T(8,128)(2,1)S(1)} %get-tuple-element.54), channel_id=1, source_target_pairs={{8,0},{16,8},{24,16},{32,24},{40,32},{48,40},{56,48},{64,56},{72,6... | collective-permute-start | bytes 147464 | tf_op jit(solution)/shard_map/ppermute | solution.py:35
  81.9 6.0 %collective-permute-start.3 = (bf16[6,18,1,128]{3,2,1,0:T(2,128)(2,1)S(1)}, bf16[6,18,1,128]{3,2,1,0:T(2,128)(2,1)S(1)}, u32[]{:S(2)}, u32[]{:S(2)}) collective-permute-start(bf16[6,18,1,128]{3,2,1,0:T(2,128)(2,1)S(1)} %get-tuple-element.49), channel_id=1, source_target_pairs={{0,1},{1,2},{2,3},{3,4},{4,5},{5,6},{6,7},{8,9},{9,10},{10,11},{11... | collective-permute-start | bytes 82952 | tf_op jit(solution)/shard_map/ppermute | solution.py:33
  85.8 5.5 %collective-permute-start.4 = (bf16[6,18,1,128]{3,2,1,0:T(2,128)(2,1)S(1)}, bf16[6,18,1,128]{3,2,1,0:T(2,128)(2,1)S(1)}, u32[]{:S(2)}, u32[]{:S(2)}) collective-permute-start(bf16[6,18,1,128]{3,2,1,0:T(2,128)(2,1)S(1)} %get-tuple-element.50), channel_id=1, source_target_pairs={{1,0},{2,1},{3,2},{4,3},{5,4},{6,5},{7,6},{9,8},{10,9},{11,10},{12... | collective-permute-start | bytes 82952 | tf_op jit(solution)/shard_map/ppermute | solution.py:35
  95.8 2.2 %copy-start.1 = (bf16[3,3,3,128,128]{4,3,2,1,0:T(8,128)(2,1)S(1)}, bf16[3,3,3,128,128]{4,3,2,1,0:T(8,128)(2,1)}, u32[]{:S(2)}) copy-start(bf16[3,3,3,128,128]{4,3,2,1,0:T(8,128)(2,1)} %param.10) | copy-start | bytes 2654212
  102.6 44.2 %copy-start.3 = (f32[128]{0:T(128)S(1)}, f32[128]{0:T(128)}, u32[]{:S(2)}) copy-start(f32[128]{0:T(128)} %param.12) | copy-start | bytes 1540
  102.6 44.2 %copy-start.4 = (f32[128]{0:T(128)S(1)}, f32[128]{0:T(128)}, u32[]{:S(2)}) copy-start(f32[128]{0:T(128)} %param.11) | copy-start | bytes 1540
  147.2 6.9 %collective-permute-start.5 = (bf16[2,16,32,128]{3,2,1,0:T(8,128)(2,1)S(1)}, bf16[2,16,32,128]{3,2,1,0:T(8,128)(2,1)S(1)}, u32[]{:S(2)}, u32[]{:S(2)}) collective-permute-start(bf16[2,16,32,128]{3,2,1,0:T(8,128)(2,1)S(1)} %slice.223), channel_id=1, source_target_pairs={{0,128},{128,256},{256,384},{1,129},{129,257},{257,385},{2,130},{1... | collective-permute-start | bytes 786440 | tf_op jit(solution)/shard_map/ppermute | solution.py:22
  154.1 11.4 %collective-permute-start.6 = (bf16[6,1,32,128]{3,2,1,0:T(8,128)(2,1)S(1)}, bf16[6,1,32,128]{3,2,1,0:T(8,128)(2,1)S(1)}, u32[]{:S(2)}, u32[]{:S(2)}) collective-permute-start(bf16[6,1,32,128]{3,2,1,0:T(8,128)(2,1)S(1)} %get-tuple-element.51), channel_id=1, source_target_pairs={{0,8},{8,16},{16,24},{24,32},{32,40},{40,48},{48,56},{56,64},{64,7... | collective-permute-start | bytes 147464 | tf_op jit(solution)/shard_map/ppermute | solution.py:33
  163.6 10.9 %collective-permute-start.7 = (bf16[6,1,32,128]{3,2,1,0:T(8,128)(2,1)S(1)}, bf16[6,1,32,128]{3,2,1,0:T(8,128)(2,1)S(1)}, u32[]{:S(2)}, u32[]{:S(2)}) collective-permute-start(bf16[6,1,32,128]{3,2,1,0:T(8,128)(2,1)S(1)} %get-tuple-element.52), channel_id=1, source_target_pairs={{8,0},{16,8},{24,16},{32,24},{40,32},{48,40},{56,48},{64,56},{72,6... | collective-permute-start | bytes 147464 | tf_op jit(solution)/shard_map/ppermute | solution.py:35
  174.5 9.2 %collective-permute-start.8 = (bf16[6,18,1,128]{3,2,1,0:T(2,128)(2,1)S(1)}, bf16[6,18,1,128]{3,2,1,0:T(2,128)(2,1)S(1)}, u32[]{:S(2)}, u32[]{:S(2)}) collective-permute-start(bf16[6,18,1,128]{3,2,1,0:T(2,128)(2,1)S(1)} %get-tuple-element.47), channel_id=1, source_target_pairs={{0,1},{1,2},{2,3},{3,4},{4,5},{5,6},{6,7},{8,9},{9,10},{10,11},{11... | collective-permute-start | bytes 82952 | tf_op jit(solution)/shard_map/ppermute | solution.py:33
  181.7 5.5 %collective-permute-start.9 = (bf16[6,18,1,128]{3,2,1,0:T(2,128)(2,1)S(1)}, bf16[6,18,1,128]{3,2,1,0:T(2,128)(2,1)S(1)}, u32[]{:S(2)}, u32[]{:S(2)}) collective-permute-start(bf16[6,18,1,128]{3,2,1,0:T(2,128)(2,1)S(1)} %get-tuple-element.48), channel_id=1, source_target_pairs={{1,0},{2,1},{3,2},{4,3},{5,4},{6,5},{7,6},{9,8},{10,9},{11,10},{12... | collective-permute-start | bytes 82952 | tf_op jit(solution)/shard_map/ppermute | solution.py:35
  191.6 2.2 %copy-start.2 = (bf16[3,3,3,128,128]{4,3,2,1,0:T(8,128)(2,1)S(1)}, bf16[3,3,3,128,128]{4,3,2,1,0:T(8,128)(2,1)}, u32[]{:S(2)}) copy-start(bf16[3,3,3,128,128]{4,3,2,1,0:T(8,128)(2,1)} %param.13) | copy-start | bytes 2654212
  198.5 1.0 copy-start
where the time goes:
time: 201 us; the launch traced here: 200 us
  blocking collectives  94.8 us (47%)
  starting transfers between devices  39.6 us (20%)
  waiting for transfers between devices  35.4 us (18%)
  other arithmetic  13.7 us (7%)
  matrix products  10.8 us (5%)
  local copies, waits for them, and re-layouts  5.8 us (3%)
    psum x10, blocking collectives, by_axis(): value = lax.psum(value, axis)  94.8 us
    ppermute x4, starting transfers between devices, extended(): lax.ppermute(tail, axis, [(i, (i + 1) % count) for i in range(ends)])  28.6 us
    ppermute x4, waiting for transfers between devices, extended(): lax.ppermute(head, axis, [((i + 1) % count, i) for i in range(ends)])  24.6 us
    ppermute x2, waiting for transfers between devices, passed_along(): lax.ppermute(value, axis, [(source, source + steps) for source in range(i...  10.9 us
    dot_general x18, matrix products, causal_conv(): jnp.dot(window, taps[dt, dh], preferred_element_type=jnp.float32)  10.8 us
    concatenate x2, other arithmetic, causal_conv(): jnp.concatenate([padded[:, :, d:d + cols, :] for d in range(3)], axis=-1)  8.93 us
    ppermute x4, starting transfers between devices, extended(): lax.ppermute(head, axis, [((i + 1) % count, i) for i in range(ends)])  8.01 us
    slice x2, local copies, waits for them, and re-layouts, causal_conv(): window = stacked[dt:dt + frames, dh:dh + rows].reshape(-1, 3 * chans)  4.44 us
  transfers between devices with their start and end apart: 10, of which 6 were waited for; matrix products, arithmetic and copies ran while one was open for 0% of the time, Pallas kernels for 0%

commit v1 on v0

v1 whole, which is shorter than its diff:
```python
import jax
import jax.numpy as jnp
from jax import lax
from jax.sharding import Mesh
from jax.sharding import PartitionSpec as P

GROUPS = 32
TH = ("th_0", "th_1")
TW = ("tw_0", "tw_1")


def gathered_sum(value, axis):
    return jnp.sum(lax.all_gather(value, axis), axis=0)


def shifted(value, axis, step):
    count = lax.axis_size(axis)
    pairs = [(i, i + step) for i in range(count) if 0 <= i + step < count]
    return lax.ppermute(value, axis, pairs)


def extended_and_summed(block, sums):
    before = shifted(block[-2:], "section", 1)
    sums = gathered_sum(sums, "th_0")
    before, sums = lax.optimization_barrier((before, sums))
    left = shifted(jnp.concatenate([before[:, :, -1:], block[:, :, -1:]], 0), TW, 1)
    right = shifted(jnp.concatenate([before[:, :, :1], block[:, :, :1]], 0), TW, -1)
    sums = gathered_sum(gathered_sum(sums, "tw_0"), "tw_1")
    left, right, sums = lax.optimization_barrier((left, right, sums))
    wide = jnp.concatenate([left, jnp.concatenate([before, block], 0), right], 2)
    above = shifted(wide[:, -1:], TH, 1)
    below = shifted(wide[:, :1], TH, -1)
    sums = gathered_sum(gathered_sum(sums, "th_1"), "section")
    above, below, sums = lax.optimization_barrier((above, below, sums))
    return jnp.concatenate([above, wide, below], 1), sums


def inside(shape):
    frame = lax.broadcasted_iota(jnp.int32, shape, 0) + 4 * lax.axis_index("section")
    row = lax.broadcasted_iota(jnp.int32, shape, 1) + 16 * lax.axis_index(TH)
    col = lax.broadcasted_iota(jnp.int32, shape, 2) + 32 * lax.axis_index(TW)
    return (frame >= 2) & (row >= 1) & (row <= 256) & (col >= 1) & (col <= 256)


def local_sums(values):
    flat = values.reshape(-1, values.shape[-1])
    return jnp.concatenate([jnp.sum(flat, 0), jnp.sum(flat * flat, 0)])[None]


def scale_and_offset(sums, count, gain, shift):
    per = sums.shape[-1] // 2 // GROUPS
    totals = jnp.sum(sums.reshape(2, GROUPS, per), -1) / count
    mean = jnp.repeat(totals[0], per)
    var = jnp.repeat(totals[1] - totals[0] * totals[0], per)
    scale = gain / jnp.sqrt(var + 1e-06)
    return scale, shift - mean * scale


def activated(block, own, gain, shift):
    count = own.size // GROUPS * 512
    full, sums = extended_and_summed(block, local_sums(own))
    scale, offset = scale_and_offset(sums, count, gain, shift)
    act = jax.nn.silu(full.astype(jnp.float32) * scale + offset)
    return jnp.where(inside(full.shape[:3] + (1,)), act, 0).astype(jnp.bfloat16)


def causal_conv(padded, kernel):
    frames = padded.shape[0] - 2
    rows = padded.shape[1] - 2
    cols = padded.shape[2] - 2
    chans = padded.shape[3]
    stacked = jnp.concatenate([padded[:, :, d : d + cols, :] for d in range(3)], axis=-1)
    taps = kernel.reshape(3, 3, 3 * chans, kernel.shape[-1])
    total = jnp.zeros((frames * rows * cols, kernel.shape[-1]), jnp.float32)
    for dt in range(3):
        for dh in range(3):
            window = stacked[dt : dt + frames, dh : dh + rows].reshape(-1, 3 * chans)
            total = total + jnp.dot(window, taps[dt, dh], preferred_element_type=jnp.float32)
    return total.reshape(frames, rows, cols, kernel.shape[-1])


def shards(features, norm_gain, norm_shift, first_kernel, second_gain, second_shift, second_kernel):
    inputs = features.astype(jnp.float32)
    first_act = activated(features, inputs, norm_gain, norm_shift)
    hidden = causal_conv(first_act, first_kernel)
    second_act = activated(hidden.astype(jnp.bfloat16), hidden, second_gain, second_shift)
    branch = causal_conv(second_act, second_kernel)
    return (inputs + branch).astype(jnp.bfloat16)


def solution(mesh):
    torus = Mesh(
        mesh.devices.reshape(mesh.shape["section"], 4, 4, 4, 2),
        ("section", "th_0", "th_1", "tw_0", "tw_1"),
    )
    return jax.shard_map(
        shards,
        mesh=torus,
        in_specs=(P("section", TH, TW, None), P(), P(), P(), P(), P(), P()),
        out_specs=P("section", TH, TW, None),
        check_vma=False,
    )
```

time: 201 us -> 157 us (0.78)
  the two profiles are of different devices: /device:TPU:25 before, /device:TPU:34 now
where the time goes in v1:
time: 157 us
  blocking collectives  99.9 us (64%)
  starting transfers between devices  27.3 us (17%)
  matrix products  10.4 us (7%)
  other arithmetic  9.54 us (6%)
  local copies, waits for them, and re-layouts  8.73 us (6%)
    all_gather x10, blocking collectives, gathered_sum(): return jnp.sum(lax.all_gather(value, axis), axis=0)  99.9 us
    ppermute x10, starting transfers between devices, shifted(): return lax.ppermute(value, axis, pairs)  27.3 us
    dot_general x18, matrix products, causal_conv(): jnp.dot(window, taps[dt, dh], preferred_element_type=jnp.float32)  10.4 us
    convert_element_type x2, other arithmetic, activated(): return jnp.where(inside(full.shape[:3] + (1,)), act, 0).astype(jnp.bfloat16)  4.44 us
    slice x2, local copies, waits for them, and re-layouts, causal_conv(): window = stacked[dt:dt + frames, dh:dh + rows].reshape(-1, 3 * chans)  4.32 us
  transfers between devices with their start and end apart: 10, of which 0 were waited for; matrix products, arithmetic and copies ran while one was open for 1% of the time, Pallas kernels for 0%

profile of v1, /device:TPU:34, one launch (start us, length us, event | category | flops | bytes accessed | tf_op | source)
XLA Modules:
  0.0 156.6 jit_solution(12069386485502826283)
XLA Ops:
  0.0 1.0 slice.187
  1.2 3.8 %collective-permute-start = (bf16[2,16,32,128]{3,1,2,0:T(8,128)(2,1)S(1)}, bf16[2,16,32,128]{3,1,2,0:T(8,128)(2,1)S(1)}, u32[]{:S(2)}, u32[]{:S(2)}) collective-permute-start(bf16[2,16,32,128]{3,1,2,0:T(8,128)(2,1)S(1)} %copy.19), channel_id=1, source_target_pairs={{0,128},{128,256},{256,384},{1,129},{129,257},{257,385},{2,130},{1... | collective-permute-start | bytes 786440 | tf_op jit(solution)/shard_map/ppermute | solution.py:19
  5.0 1.3 convert_reduce_fusion
  6.5 18.7 %all-gather.10 = f32[4,1,256]{2,1,0:T(1,128)S(1)} all-gather(f32[1,1,256]{2,1,0:T(1,128)S(1)} %bitcast.176), channel_id=2, replica_groups=mesh['section'=4,'th_0'=4,'th_1'=4,'tw_0'=4,'tw_1'=2] {'th_0'}, dimensions={0}, use_global_device_ids=true | all-gather | bytes 5120 | tf_op jit(solution)/shard_map/all_gather | solution.py:13
  25.3 1.9 %collective-permute-start.1 = (bf16[6,16,1,128]{3,1,2,0:T(8,128)(2,1)S(1)}, bf16[6,16,1,128]{3,1,2,0:T(8,128)(2,1)S(1)}, u32[]{:S(2)}, u32[]{:S(2)}) collective-permute-start(bf16[6,16,1,128]{3,1,2,0:T(8,128)(2,1)S(1)} %pad_maximum_fusion.11), channel_id=1, source_target_pairs={{0,1},{1,2},{2,3},{3,4},{4,5},{5,6},{6,7},{8,9},{9,10},{10,11},{11... | collective-permute-start | bytes 73736 | tf_op jit(solution)/shard_map/ppermute | solution.py:19
  27.2 3.6 %collective-permute-start.2 = (bf16[6,16,1,128]{3,1,2,0:T(8,128)(2,1)S(1)}, bf16[6,16,1,128]{3,1,2,0:T(8,128)(2,1)S(1)}, u32[]{:S(2)}, u32[]{:S(2)}) collective-permute-start(bf16[6,16,1,128]{3,1,2,0:T(8,128)(2,1)S(1)} %pad_maximum_fusion.12), channel_id=1, source_target_pairs={{1,0},{2,1},{3,2},{4,3},{5,4},{6,5},{7,6},{9,8},{10,9},{11,10},{12... | collective-permute-start | bytes 73736 | tf_op jit(solution)/shard_map/ppermute | solution.py:19
  31.0 7.9 %all-gather.11 = f32[4,1,256]{2,1,0:T(1,128)S(1)} all-gather(f32[1,1,256]{2,1,0:T(1,128)S(1)} %bitcast.178), channel_id=3, replica_groups=mesh['section'=4,'th_0'=4,'th_1'=4,'tw_0'=4,'tw_1'=2] {'tw_0'}, dimensions={0}, use_global_device_ids=true | all-gather | bytes 5120 | tf_op jit(solution)/shard_map/all_gather | solution.py:13
  38.8 1.8 %all-gather.12 = f32[2,1,256]{2,1,0:T(1,128)S(1)} all-gather(f32[1,1,256]{2,1,0:T(1,128)S(1)} %bitcast.180), channel_id=4, replica_groups=mesh['section'=4,'th_0'=4,'th_1'=4,'tw_0'=4,'tw_1'=2] {'tw_1'}, dimensions={0}, use_global_device_ids=true | all-gather | bytes 3072 | tf_op jit(solution)/shard_map/all_gather | solution.py:13
  40.8 1.3 collective-permute-start.4
  42.1 4.5 %collective-permute-start.3 = (bf16[6,1,34,128]{3,2,1,0:T(8,128)(2,1)S(1)}, bf16[6,1,34,128]{3,2,1,0:T(8,128)(2,1)S(1)}, u32[]{:S(2)}, u32[]{:S(2)}) collective-permute-start(bf16[6,1,34,128]{3,2,1,0:T(8,128)(2,1)S(1)} %get-tuple-element.73), channel_id=1, source_target_pairs={{0,8},{8,16},{16,24},{24,32},{32,40},{40,48},{48,56},{56,64},{64,7... | collective-permute-start | bytes 156680 | tf_op jit(solution)/shard_map/ppermute | solution.py:19
  46.8 16.0 %all-gather.13 = f32[4,1,256]{2,1,0:T(1,128)S(1)} all-gather(f32[1,1,256]{2,1,0:T(1,128)S(1)} %bitcast.174), channel_id=5, replica_groups=mesh['section'=4,'th_0'=4,'th_1'=4,'tw_0'=4,'tw_1'=2] {'th_1'}, dimensions={0}, use_global_device_ids=true | all-gather | bytes 5120 | tf_op jit(solution)/shard_map/all_gather | solution.py:13
  62.8 8.6 %all-gather.14 = f32[4,1,256]{2,1,0:T(1,128)S(1)} all-gather(f32[1,1,256]{2,1,0:T(1,128)S(1)} %bitcast.181), channel_id=6, replica_groups=mesh['section'=4,'th_0'=4,'th_1'=4,'tw_0'=4,'tw_1'=2] {'section'}, dimensions={0}, use_global_device_ids=true | all-gather | bytes 5120 | tf_op jit(solution)/shard_map/all_gather | solution.py:13
  72.0 0.7 reduce.42
  73.3 2.2 %select_convert_fusion.1 = bf16[6,18,34,128]{3,2,1,0:T(8,128)(2,1)S(1)} fusion(bf16[6,1,34,128]{3,2,1,0:T(8,128)(2,1)S(1)} %collective-permute-done.4, bf16[6,16,1,128]{3,2,1,0:T(2,128)(2,1)S(1)} %copy.13, bf16[4,16,32,128]{3,2,1,0:T(8,128)(2,1)S(1)} %copy-done, bf16[2,16,32,128]{3,2,1,0:T(8,128)(2,1)S(1)} %copy.11, bf16[6,16,1,128]{3,2,1,0:T(2,128)(2,1)S(1)} %copy.12, ...), kind=kLoop, calls=%fused_computation.19 | loop fusion | flops 9400320 | bytes 1884760 | tf_op jit(solution)/shard_map/convert_element_type | solution.py:64
  75.5 0.6 fusion.16
  76.5 2.2 %fusion.14 = (bf16[4,16,32,384]{3,2,1,0:T(8,128)(2,1)S(1)}, bf16[4,16,32,384]{3,2,1,0:T(8,128)(2,1)S(1)}, bf16[4,16,32,384]{3,2,1,0:T(8,128)(2,1)S(1)}, bf16[4,1...) fusion(bf16[6,18,32,384]{3,2,1,0:T(8,128)(2,1)S(1)} %pad_maximu, ...), kind=kLoop, calls=%fused_computation.82 | loop fusion | bytes 28311552 | tf_op jit(solution)/shard_map/slice | solution.py:77
  83.3 0.7 fusion.12
  84.1 1.9 %collective-permute-start.5 = (bf16[2,16,32,128]{3,1,2,0:T(8,128)(2,1)S(1)}, bf16[2,16,32,128]{3,1,2,0:T(8,128)(2,1)S(1)}, u32[]{:S(2)}, u32[]{:S(2)}) collective-permute-start(bf16[2,16,32,128]{3,1,2,0:T(8,128)(2,1)S(1)} %copy.14), channel_id=1, source_target_pairs={{0,128},{128,256},{256,384},{1,129},{129,257},{257,385},{2,130},{1... | collective-permute-start | bytes 786440 | tf_op jit(solution)/shard_map/ppermute | solution.py:19
  86.1 13.2 %all-gather.15 = f32[4,1,256]{2,1,0:T(1,128)S(1)} all-gather(f32[1,1,256]{2,1,0:T(1,128)S(1)} %bitcast.177), channel_id=7, replica_groups=mesh['section'=4,'th_0'=4,'th_1'=4,'tw_0'=4,'tw_1'=2] {'th_0'}, dimensions={0}, use_global_device_ids=true | all-gather | bytes 5120 | tf_op jit(solution)/shard_map/all_gather | solution.py:13
  99.5 1.9 %collective-permute-start.7 = (bf16[6,16,1,128]{3,1,2,0:T(8,128)(2,1)S(1)}, bf16[6,16,1,128]{3,1,2,0:T(8,128)(2,1)S(1)}, u32[]{:S(2)}, u32[]{:S(2)}) collective-permute-start(bf16[6,16,1,128]{3,1,2,0:T(8,128)(2,1)S(1)} %pad_maximum_fusion.13), channel_id=1, source_target_pairs={{1,0},{2,1},{3,2},{4,3},{5,4},{6,5},{7,6},{9,8},{10,9},{11,10},{12... | collective-permute-start | bytes 73736 | tf_op jit(solution)/shard_map/ppermute | solution.py:19
  101.5 2.4 %collective-permute-start.6 = (bf16[6,16,1,128]{3,2,1,0:T(2,128)(2,1)S(1)}, bf16[6,16,1,128]{3,2,1,0:T(2,128)(2,1)S(1)}, u32[]{:S(2)}, u32[]{:S(2)}) collective-permute-start(bf16[6,16,1,128]{3,2,1,0:T(2,128)(2,1)S(1)} %pad_maximum_fusion.10), channel_id=1, source_target_pairs={{0,1},{1,2},{2,3},{3,4},{4,5},{5,6},{6,7},{8,9},{9,10},{10,11},{11... | collective-permute-start | bytes 73736 | tf_op jit(solution)/shard_map/ppermute | solution.py:19
  103.9 9.4 %all-gather.16 = f32[4,1,256]{2,1,0:T(1,128)S(1)} all-gather(f32[1,1,256]{2,1,0:T(1,128)S(1)} %bitcast.179), channel_id=8, replica_groups=mesh['section'=4,'th_0'=4,'th_1'=4,'tw_0'=4,'tw_1'=2] {'tw_0'}, dimensions={0}, use_global_device_ids=true | all-gather | bytes 5120 | tf_op jit(solution)/shard_map/all_gather | solution.py:13
  113.4 1.8 %all-gather.17 = f32[2,1,256]{2,1,0:T(1,128)S(1)} all-gather(f32[1,1,256]{2,1,0:T(1,128)S(1)} %bitcast.182), channel_id=9, replica_groups=mesh['section'=4,'th_0'=4,'th_1'=4,'tw_0'=4,'tw_1'=2] {'tw_1'}, dimensions={0}, use_global_device_ids=true | all-gather | bytes 3072 | tf_op jit(solution)/shard_map/all_gather | solution.py:13
  115.3 1.3 collective-permute-start.9
  116.6 4.5 %collective-permute-start.8 = (bf16[6,1,34,128]{3,2,1,0:T(8,128)(2,1)S(1)}, bf16[6,1,34,128]{3,2,1,0:T(8,128)(2,1)S(1)}, u32[]{:S(2)}, u32[]{:S(2)}) collective-permute-start(bf16[6,1,34,128]{3,2,1,0:T(8,128)(2,1)S(1)} %get-tuple-element.71), channel_id=1, source_target_pairs={{0,8},{8,16},{16,24},{24,32},{32,40},{40,48},{48,56},{56,64},{64,7... | collective-permute-start | bytes 156680 | tf_op jit(solution)/shard_map/ppermute | solution.py:19
  121.2 12.7 %all-gather.18 = f32[4,1,256]{2,1,0:T(1,128)S(1)} all-gather(f32[1,1,256]{2,1,0:T(1,128)S(1)} %bitcast.175), channel_id=10, replica_groups=mesh['section'=4,'th_0'=4,'th_1'=4,'tw_0'=4,'tw_1'=2] {'th_1'}, dimensions={0}, use_global_device_ids=true | all-gather | bytes 5120 | tf_op jit(solution)/shard_map/all_gather | solution.py:13
  133.9 9.8 %all-gather.19 = f32[4,1,256]{2,1,0:T(1,128)S(1)} all-gather(f32[1,1,256]{2,1,0:T(1,128)S(1)} %bitcast.183), channel_id=11, replica_groups=mesh['section'=4,'th_0'=4,'th_1'=4,'tw_0'=4,'tw_1'=2] {'section'}, dimensions={0}, use_global_device_ids=true | all-gather | bytes 5120 | tf_op jit(solution)/shard_map/all_gather | solution.py:13
  143.8 0.7 reduce.43
  145.1 2.2 %select_convert_fusion = bf16[6,18,34,128]{3,2,1,0:T(8,128)(2,1)S(1)} fusion(bf16[6,1,34,128]{3,2,1,0:T(8,128)(2,1)S(1)} %collective-permute-done.9, bf16[6,16,1,128]{3,2,1,0:T(2,128)(2,1)S(1)} %copy.18, bf16[4,16,32,128]{3,2,1,0:T(8,128)(2,1)S(1)} %bitcast.135, bf16[2,16,32,128]{3,2,1,0:T(8,128)(2,1)S(1)} %copy.17, ...), kind=kLoop, calls=%fused_computation.18 | loop fusion | flops 9400320 | bytes 1884760 | tf_op jit(solution)/shard_map/convert_element_type | solution.py:64
  147.3 0.6 fusion.15
  148.3 2.2 %fusion.13 = (bf16[4,16,32,384]{3,2,1,0:T(8,128)(2,1)S(1)}, bf16[4,16,32,384]{3,2,1,0:T(8,128)(2,1)S(1)}, bf16[4,16,32,384]{3,2,1,0:T(8,128)(2,1)S(1)}, bf16[4,1...) fusion(bf16[6,18,32,384]{3,2,1,0:T(8,128)(2,1)S(1)} %pad_maximu, ...), kind=kLoop, calls=%fused_computation.81 | loop fusion | bytes 28311552 | tf_op jit(solution)/shard_map/slice | solution.py:77
  155.7 0.9 fusion.1
  (102 shorter events, 13.4 us)
Async XLA Ops:
  0.0 6.3 %copy-start = (bf16[4,16,32,128]{3,2,1,0:T(8,128)(2,1)S(1)}, bf16[4,16,32,128]{3,2,1,0:T(8,128)(2,1)}, u32[]{:S(2)}) copy-start(bf16[4,16,32,128]{3,2,1,0:T(8,128)(2,1)} %param.7) | copy-start | bytes 1572868
  1.0 72.2 %copy-start.3 = (f32[128]{0:T(128)S(1)}, f32[128]{0:T(128)}, u32[]{:S(2)}) copy-start(f32[128]{0:T(128)} %param.9) | copy-start | bytes 1540
  1.1 72.2 %copy-start.4 = (f32[128]{0:T(128)S(1)}, f32[128]{0:T(128)}, u32[]{:S(2)}) copy-start(f32[128]{0:T(128)} %param.8) | copy-start | bytes 1540
  1.2 24.1 %collective-permute-start = (bf16[2,16,32,128]{3,1,2,0:T(8,128)(2,1)S(1)}, bf16[2,16,32,128]{3,1,2,0:T(8,128)(2,1)S(1)}, u32[]{:S(2)}, u32[]{:S(2)}) collective-permute-start(bf16[2,16,32,128]{3,1,2,0:T(8,128)(2,1)S(1)} %copy.19), channel_id=1, source_target_pairs={{0,128},{128,256},{256,384},{1,129},{129,257},{257,385},{2,130},{1... | collective-permute-start | bytes 786440 | tf_op jit(solution)/shard_map/ppermute | solution.py:19
  25.3 15.4 %collective-permute-start.1 = (bf16[6,16,1,128]{3,1,2,0:T(8,128)(2,1)S(1)}, bf16[6,16,1,128]{3,1,2,0:T(8,128)(2,1)S(1)}, u32[]{:S(2)}, u32[]{:S(2)}) collective-permute-start(bf16[6,16,1,128]{3,1,2,0:T(8,128)(2,1)S(1)} %pad_maximum_fusion.11), channel_id=1, source_target_pairs={{0,1},{1,2},{2,3},{3,4},{4,5},{5,6},{6,7},{8,9},{9,10},{10,11},{11... | collective-permute-start | bytes 73736 | tf_op jit(solution)/shard_map/ppermute | solution.py:19
  27.2 13.5 %collective-permute-start.2 = (bf16[6,16,1,128]{3,1,2,0:T(8,128)(2,1)S(1)}, bf16[6,16,1,128]{3,1,2,0:T(8,128)(2,1)S(1)}, u32[]{:S(2)}, u32[]{:S(2)}) collective-permute-start(bf16[6,16,1,128]{3,1,2,0:T(8,128)(2,1)S(1)} %pad_maximum_fusion.12), channel_id=1, source_target_pairs={{1,0},{2,1},{3,2},{4,3},{5,4},{6,5},{7,6},{9,8},{10,9},{11,10},{12... | collective-permute-start | bytes 73736 | tf_op jit(solution)/shard_map/ppermute | solution.py:19
  40.8 30.6 %collective-permute-start.4 = (bf16[6,1,34,128]{3,2,1,0:T(8,128)(2,1)S(1)}, bf16[6,1,34,128]{3,2,1,0:T(8,128)(2,1)S(1)}, u32[]{:S(2)}, u32[]{:S(2)}) collective-permute-start(bf16[6,1,34,128]{3,2,1,0:T(8,128)(2,1)S(1)} %get-tuple-element.72), channel_id=1, source_target_pairs={{8,0},{16,8},{24,16},{32,24},{40,32},{48,40},{56,48},{64,56},{72,6... | collective-permute-start | bytes 156680 | tf_op jit(solution)/shard_map/ppermute | solution.py:19
  42.1 29.3 %collective-permute-start.3 = (bf16[6,1,34,128]{3,2,1,0:T(8,128)(2,1)S(1)}, bf16[6,1,34,128]{3,2,1,0:T(8,128)(2,1)S(1)}, u32[]{:S(2)}, u32[]{:S(2)}) collective-permute-start(bf16[6,1,34,128]{3,2,1,0:T(8,128)(2,1)S(1)} %get-tuple-element.73), channel_id=1, source_target_pairs={{0,8},{8,16},{16,24},{24,32},{32,40},{40,48},{48,56},{56,64},{64,7... | collective-permute-start | bytes 156680 | tf_op jit(solution)/shard_map/ppermute | solution.py:19
  76.5 2.2 %copy-start.1 = (bf16[3,3,3,128,128]{4,3,2,1,0:T(8,128)(2,1)S(1)}, bf16[3,3,3,128,128]{4,3,2,1,0:T(8,128)(2,1)}, u32[]{:S(2)}) copy-start(bf16[3,3,3,128,128]{4,3,2,1,0:T(8,128)(2,1)} %param.10) | copy-start | bytes 2654212
  84.0 61.0 %copy-start.5 = (f32[128]{0:T(128)S(1)}, f32[128]{0:T(128)}, u32[]{:S(2)}) copy-start(f32[128]{0:T(128)} %param.12) | copy-start | bytes 1540
  84.0 61.1 %copy-start.6 = (f32[128]{0:T(128)S(1)}, f32[128]{0:T(128)}, u32[]{:S(2)}) copy-start(f32[128]{0:T(128)} %param.11) | copy-start | bytes 1540
  84.1 15.3 %collective-permute-start.5 = (bf16[2,16,32,128]{3,1,2,0:T(8,128)(2,1)S(1)}, bf16[2,16,32,128]{3,1,2,0:T(8,128)(2,1)S(1)}, u32[]{:S(2)}, u32[]{:S(2)}) collective-permute-start(bf16[2,16,32,128]{3,1,2,0:T(8,128)(2,1)S(1)} %copy.14), channel_id=1, source_target_pairs={{0,128},{128,256},{256,384},{1,129},{129,257},{257,385},{2,130},{1... | collective-permute-start | bytes 786440 | tf_op jit(solution)/shard_map/ppermute | solution.py:19
  99.5 15.7 %collective-permute-start.7 = (bf16[6,16,1,128]{3,1,2,0:T(8,128)(2,1)S(1)}, bf16[6,16,1,128]{3,1,2,0:T(8,128)(2,1)S(1)}, u32[]{:S(2)}, u32[]{:S(2)}) collective-permute-start(bf16[6,16,1,128]{3,1,2,0:T(8,128)(2,1)S(1)} %pad_maximum_fusion.13), channel_id=1, source_target_pairs={{1,0},{2,1},{3,2},{4,3},{5,4},{6,5},{7,6},{9,8},{10,9},{11,10},{12... | collective-permute-start | bytes 73736 | tf_op jit(solution)/shard_map/ppermute | solution.py:19
  101.5 13.7 %collective-permute-start.6 = (bf16[6,16,1,128]{3,2,1,0:T(2,128)(2,1)S(1)}, bf16[6,16,1,128]{3,2,1,0:T(2,128)(2,1)S(1)}, u32[]{:S(2)}, u32[]{:S(2)}) collective-permute-start(bf16[6,16,1,128]{3,2,1,0:T(2,128)(2,1)S(1)} %pad_maximum_fusion.10), channel_id=1, source_target_pairs={{0,1},{1,2},{2,3},{3,4},{4,5},{5,6},{6,7},{8,9},{9,10},{10,11},{11... | collective-permute-start | bytes 73736 | tf_op jit(solution)/shard_map/ppermute | solution.py:19
  115.3 28.4 %collective-permute-start.9 = (bf16[6,1,34,128]{3,2,1,0:T(8,128)(2,1)S(1)}, bf16[6,1,34,128]{3,2,1,0:T(8,128)(2,1)S(1)}, u32[]{:S(2)}, u32[]{:S(2)}) collective-permute-start(bf16[6,1,34,128]{3,2,1,0:T(8,128)(2,1)S(1)} %get-tuple-element.70), channel_id=1, source_target_pairs={{8,0},{16,8},{24,16},{32,24},{40,32},{48,40},{56,48},{64,56},{72,6... | collective-permute-start | bytes 156680 | tf_op jit(solution)/shard_map/ppermute | solution.py:19
  116.6 27.1 %collective-permute-start.8 = (bf16[6,1,34,128]{3,2,1,0:T(8,128)(2,1)S(1)}, bf16[6,1,34,128]{3,2,1,0:T(8,128)(2,1)S(1)}, u32[]{:S(2)}, u32[]{:S(2)}) collective-permute-start(bf16[6,1,34,128]{3,2,1,0:T(8,128)(2,1)S(1)} %get-tuple-element.71), channel_id=1, source_target_pairs={{0,8},{8,16},{16,24},{24,32},{32,40},{40,48},{48,56},{56,64},{64,7... | collective-permute-start | bytes 156680 | tf_op jit(solution)/shard_map/ppermute | solution.py:19
  148.3 2.2 %copy-start.2 = (bf16[3,3,3,128,128]{4,3,2,1,0:T(8,128)(2,1)S(1)}, bf16[3,3,3,128,128]{4,3,2,1,0:T(8,128)(2,1)}, u32[]{:S(2)}) copy-start(bf16[3,3,3,128,128]{4,3,2,1,0:T(8,128)(2,1)} %param.13) | copy-start | bytes 2654212

commit v2 on v1

v2 whole, which is shorter than its diff:
```python
import functools

import jax
import jax.numpy as jnp
from jax import lax
from jax.experimental import pallas as pl
from jax.experimental.pallas import tpu as pltpu
from jax.sharding import Mesh
from jax.sharding import PartitionSpec as P

TH = ("th_0", "th_1")
TW = ("tw_0", "tw_1")
PER = 4
CHUNK = 8
EPS = 1e-06
VMEM = 20 * 2**20
F32 = jnp.float32
BF16 = jnp.bfloat16


def gathered_sum(value, axis):
    return jnp.sum(lax.all_gather(value, axis), axis=0)


def shifted(value, axis, step):
    count = lax.axis_size(axis)
    pairs = [(i, i + step) for i in range(count) if 0 <= i + step < count]
    return lax.ppermute(value, axis, pairs)


def scale_and_offset(sums_ref, gain_ref, shift_ref, count):
    totals = jnp.sum(sums_ref[...], axis=0)
    lane = lax.broadcasted_iota(jnp.int32, totals.shape, 1)
    for width in (1, 2):
        back = pltpu.roll(totals, width, 1)
        ahead = pltpu.roll(totals, totals.shape[1] - width, 1)
        totals = totals + jnp.where(lane // width % 2 == 0, ahead, back)
    totals = totals * (1.0 / count)
    mean = totals[0:1]
    var = totals[1:2] - mean * mean
    scale = gain_ref[...] / jnp.sqrt(var + EPS)
    return 0.5 * scale, 0.5 * (shift_ref[...] - mean * scale)


def silu_of_double(half):
    return half + half * jnp.tanh(half)


def edges():
    th = lax.axis_index("th_0") * lax.axis_size("th_1") + lax.axis_index("th_1")
    tw = lax.axis_index("tw_0") * lax.axis_size("tw_1") + lax.axis_index("tw_1")
    section = lax.axis_index("section")
    last_th = lax.axis_size(TH) - 1
    last_tw = lax.axis_size(TW) - 1
    tests = (section > 0, th > 0, th < last_th, tw > 0, tw < last_tw)
    return [jnp.where(t, 1.0, 0.0).astype(F32) for t in tests]


def store_act(act_ref, h, m, pairs, row_ok, before_ok, column_ok):
    ok = row_ok if column_ok is None else row_ok * column_ok
    pairs = [pairs[0] * (ok * before_ok), pairs[1] * ok, pairs[2] * ok]
    low = lax.broadcasted_iota(jnp.int32, pairs[0].shape, 0) < 4
    mid = [pltpu.roll(jnp.where(low, b, a), 4, 0) for a, b in zip(pairs[:2], pairs[1:])]
    for dt, halves in enumerate((pairs[:2], mid, pairs[1:])):
        act_ref[dt, h, m] = jnp.concatenate(halves, 0).astype(BF16)


def column_masks(left_ok, right_ok):
    chunk = lax.broadcasted_iota(jnp.int32, (8, 128), 0) % 4
    return jnp.where(chunk == 0, left_ok, 1.0), jnp.where(chunk == 3, right_ok, 1.0)


def conv_block(act_ref, kernel_ref, acc_ref, start, rows, cols):
    size = rows * cols * 16
    taps = [(dt, di, dj) for dt in range(3) for di in range(3) for dj in range(3)]
    step = 2
    for k in range(0, 27, step):
        part = taps[k : k + step]
        lhs = jnp.concatenate(
            [
                act_ref[dt, pl.ds(start + di, rows), dj : dj + cols].reshape(size, 128)
                for dt, di, dj in part
            ],
            axis=1,
        )
        rhs = kernel_ref[k * 128 : (k + len(part)) * 128, :]
        new = jnp.dot(lhs, rhs, preferred_element_type=F32)
        acc_ref[...] = new if k == 0 else acc_ref[...] + new


def prepare_body(feat_ref, last_ref, top_ref, bottom_ref, head_ref, tail_ref, sums_ref):
    last_ref[...] = feat_ref[2:4]
    top_ref[...] = feat_ref[:, 0:2]
    bottom_ref[...] = feat_ref[:, 14:16]
    head_ref[...] = feat_ref[:, :, 0:2]
    tail_ref[...] = feat_ref[:, :, 30:32]
    first = jnp.zeros((8, 128), F32)
    second = jnp.zeros((8, 128), F32)
    for t in range(4):
        for h in range(0, 16, 4):
            part = feat_ref[t, h : h + 4].astype(F32).reshape(16, 8, 128)
            first += jnp.sum(part, 0)
            second += jnp.sum(part * part, 0)
    sums_ref[0:1, :] = jnp.sum(first, 0, keepdims=True)
    sums_ref[1:2, :] = jnp.sum(second, 0, keepdims=True)


ROWS1, COLS1, BLOCK1 = 18, CHUNK + 2, 6
ROWS2, COLS2, BLOCK2 = 16, CHUNK, 8


def first_body(count, feat_ref, before_ref, above_ref, below_ref, left_ref, right_ref, sums_ref,
               gain_ref, shift_ref, kernel_ref, hidden_ref, halo_ref, out_sums_ref,
               flat_ref, act_ref, acc_ref, taps_ref, taps_sem):
    fetch = pltpu.make_async_copy(kernel_ref, taps_ref, taps_sem)
    fetch.start()
    scale, offset = scale_and_offset(sums_ref, gain_ref, shift_ref, count)
    before_ok, above_ok, below_ok, left_ok, right_ok = edges()
    left_mask, right_mask = column_masks(left_ok, right_ok)

    flat_ref[2:6, 2:18, 8:40] = feat_ref[...].astype(F32)
    flat_ref[0:2, 2:18, 8:40] = before_ref[...].astype(F32)
    flat_ref[:, 0:2, 8:40] = above_ref[...].astype(F32)
    flat_ref[:, 18:20, 8:40] = below_ref[...].astype(F32)
    flat_ref[:, :, 6:8] = left_ref[...].astype(F32)
    flat_ref[:, :, 40:42] = right_ref[...].astype(F32)

    def fill(h, _):
        row_ok = jnp.where(h < 2, above_ok, jnp.where(h >= 18, below_ok, 1.0))
        for m in range(COLS1 + 2):
            pairs = []
            for t in (0, 2, 4):
                raw = jnp.concatenate(
                    [flat_ref[t + i, h, pl.ds(6 + m, 4, stride=8), :] for i in range(2)], 0
                )
                pairs.append(silu_of_double(raw * scale + offset))
            column_ok = left_mask if m < 2 else right_mask if m >= COLS1 else None
            store_act(act_ref, h, m, pairs, row_ok, before_ok, column_ok)
        return 0

    lax.fori_loop(0, ROWS1 + 2, fill, 0)

    fetch.wait()

    def conv(b, _):
        conv_block(act_ref, taps_ref, acc_ref, b * BLOCK1, BLOCK1, COLS1)
        hidden_ref[pl.ds(b * BLOCK1, BLOCK1)] = acc_ref[...].reshape(BLOCK1, COLS1, 16, 128)
        return 0

    lax.fori_loop(0, ROWS1 // BLOCK1, conv, 0)

    def total(h, carry):
        own = hidden_ref[h, 1 : CHUNK + 1].reshape(CHUNK * 2, 8, 128)
        return carry[0] + jnp.sum(own, 0), carry[1] + jnp.sum(own * own, 0)

    zero = jnp.zeros((8, 128), F32)
    first, second = lax.fori_loop(1, ROWS1 - 1, total, (zero, zero))
    out_sums_ref[0:1, :] = jnp.sum(first, 0, keepdims=True)
    out_sums_ref[1:2, :] = jnp.sum(second, 0, keepdims=True)

    def last_frames(h, _):
        for j in range(COLS1 // 2):
            both = [hidden_ref[h, 2 * j + i, 8:16, :] for i in range(2)]
            halo_ref[h, j] = jnp.concatenate(both, 0).astype(BF16)
        return 0

    lax.fori_loop(0, ROWS1, last_frames, 0)


def second_body(count, hidden_ref, halo_ref, sums_ref, gain_ref, shift_ref, kernel_ref, feat_ref,
                out_ref, act_ref, acc_ref, flat_ref):
    scale, offset = scale_and_offset(sums_ref, gain_ref, shift_ref, count)
    before_ok, above_ok, below_ok, left_ok, right_ok = edges()
    left_mask, right_mask = column_masks(left_ok, right_ok)

    def fill(h, _):
        row_ok = jnp.where(h < 1, above_ok, jnp.where(h >= 17, below_ok, 1.0))
        for m in range(COLS2 + 2):
            halo = halo_ref[h, m // 2].astype(F32)[m % 2 * 8 : m % 2 * 8 + 8]
            raws = (halo, hidden_ref[h, m, 0:8, :], hidden_ref[h, m, 8:16, :])
            pairs = [silu_of_double(raw * scale + offset) for raw in raws]
            column_ok = left_mask if m < 1 else right_mask if m > COLS2 else None
            store_act(act_ref, h, m, pairs, row_ok, before_ok, column_ok)
        return 0

    lax.fori_loop(0, ROWS2 + 2, fill, 0)

    def conv(b, _):
        conv_block(act_ref, kernel_ref, acc_ref, b * BLOCK2, BLOCK2, COLS2)

        def spread(i, _):
            h = b * BLOCK2 + i
            for m in range(COLS2):
                tile = acc_ref[pl.ds(pl.multiple_of((i * COLS2 + m) * 16, 16), 16), :]
                for t in range(4):
                    flat_ref[t, pl.ds(m, 4, stride=8), :] = tile[4 * t : 4 * t + 4]
            for t in range(4):
                total = feat_ref[t, h].astype(F32) + flat_ref[t]
                out_ref[t, h] = total.astype(BF16)
            return 0

        lax.fori_loop(0, BLOCK2, spread, 0)
        return 0

    lax.fori_loop(0, ROWS2 // BLOCK2, conv, 0)


def in_vmem(count):
    return [pl.BlockSpec(memory_space=pltpu.VMEM)] * count


def shards(features, norm_gain, norm_shift, first_kernel, second_gain, second_shift, second_kernel):
    count = features.size // features.shape[-1] * PER
    for axis in ("section", *TH, *TW):
        count *= lax.axis_size(axis)
    last, top, bottom, head, tail, sums = pl.pallas_call(
        prepare_body,
        out_shape=tuple(
            jax.ShapeDtypeStruct(shape, BF16)
            for shape in (
                (2, 16, 32, 128), (4, 2, 32, 128), (4, 2, 32, 128), (4, 16, 2, 128), (4, 16, 2, 128)
            )
        ) + (jax.ShapeDtypeStruct((2, 128), F32),),
        in_specs=in_vmem(1),
        out_specs=tuple(in_vmem(6)),
        compiler_params=pltpu.CompilerParams(vmem_limit_bytes=VMEM),
        name="prepare",
    )(features)

    before = shifted(last, "section", 1)
    sums = gathered_sum(sums, TW)
    before, sums = lax.optimization_barrier((before, sums))
    above = shifted(jnp.concatenate([before[:, -2:], bottom], 0), TH, 1)
    below = shifted(jnp.concatenate([before[:, :2], top], 0), TH, -1)
    sums = gathered_sum(sums, "th_1")
    sums = gathered_sum(sums, "section")
    above, below, sums = lax.optimization_barrier((above, below, sums))

    def columns(own, s):
        own = jnp.concatenate([before[:, :, s], own], 0)
        return jnp.concatenate([above[:, :, s], own, below[:, :, s]], 1)

    left = shifted(columns(tail, slice(-2, None)), TW, 1)
    right = shifted(columns(head, slice(0, 2)), TW, -1)
    sums = lax.all_gather(sums, "th_0")

    hidden, halo, sums = pl.pallas_call(
        functools.partial(first_body, count),
        out_shape=(
            jax.ShapeDtypeStruct((ROWS1, COLS1, 16, 128), F32),
            jax.ShapeDtypeStruct((ROWS1, COLS1 // 2, 16, 128), BF16),
            jax.ShapeDtypeStruct((2, 128), F32),
        ),
        in_specs=[*in_vmem(9), pl.BlockSpec(memory_space=pltpu.HBM)],
        out_specs=tuple(in_vmem(3)),
        scratch_shapes=[
            pltpu.VMEM((6, 20, 48, 128), F32),
            pltpu.VMEM((3, ROWS1 + 2, COLS1 + 2, 16, 128), BF16),
            pltpu.VMEM((BLOCK1 * COLS1 * 16, 128), F32),
            pltpu.VMEM((27 * 128, 128), BF16),
            pltpu.SemaphoreType.DMA,
        ],
        compiler_params=pltpu.CompilerParams(vmem_limit_bytes=VMEM),
        name="first_conv",
    )(features, before, above, below, left, right, sums, norm_gain[None], norm_shift[None],
      pltpu.with_memory_space_constraint(first_kernel.reshape(-1, 128), pltpu.HBM))

    halo = shifted(halo, "section", 1)
    for axis in (TW, "th_1", "section"):
        sums = gathered_sum(sums, axis)
    sums = lax.all_gather(sums, "th_0")

    return pl.pallas_call(
        functools.partial(second_body, count),
        out_shape=jax.ShapeDtypeStruct(features.shape, BF16),
        in_specs=in_vmem(7),
        out_specs=in_vmem(1)[0],
        scratch_shapes=[
            pltpu.VMEM((3, ROWS2 + 2, COLS2 + 2, 16, 128), BF16),
            pltpu.VMEM((BLOCK2 * COLS2 * 16, 128), F32),
            pltpu.VMEM((4, 32, 128), F32),
        ],
        compiler_params=pltpu.CompilerParams(vmem_limit_bytes=VMEM),
        name="second_conv",
    )(hidden, halo, sums, second_gain[None], second_shift[None], second_kernel.reshape(-1, 128), features)


def solution(mesh):
    torus = Mesh(
        mesh.devices.reshape(mesh.shape["section"], 4, 4, 4, 2),
        ("section", "th_0", "th_1", "tw_0", "tw_1"),
    )
    return jax.shard_map(
        shards,
        mesh=torus,
        in_specs=(P("section", TH, TW, None), P(), P(), P(), P(), P(), P()),
        out_specs=P("section", TH, TW, None),
        check_vma=False,
    )
```

time: 157 us -> 124 us (0.79)
  the two profiles are of different devices: /device:TPU:34 before, /device:TPU:32 now
where the time goes in v2:
time: 124 us
  blocking collectives  94.2 us (76%)
  Pallas kernels  14.6 us (12%)
  starting transfers between devices  13.2 us (11%)
    all_gather x6, blocking collectives, gathered_sum(): return jnp.sum(lax.all_gather(value, axis), axis=0)  64 us
    all_gather x2, blocking collectives, shards(): sums = lax.all_gather(sums, 'th_0')  30.3 us
    ppermute x6, starting transfers between devices, shifted(): return lax.ppermute(value, axis, pairs)  13.2 us
    pallas_call x1, Pallas kernels, shards(): pl.pallas_call(functools.partial(first_body, count), out_shape=(jax.Shape...  8.32 us
    pallas_call x1, Pallas kernels, shards(): pl.pallas_call(functools.partial(second_body, count), out_shape=jax.Shape...  6.08 us
  transfers between devices with their start and end apart: 6, of which 0 were waited for; matrix products, arithmetic and copies ran while one was open for 0% of the time, Pallas kernels for 0%

profile of v2, /device:TPU:32, one launch (start us, length us, event | category | flops | bytes accessed | tf_op | source)
XLA Modules:
  0.0 123.7 jit_solution(1659251389552510265)
XLA Ops:
  0.0 1.0 copy-done
  1.0 0.2 prepare.1
  1.3 3.8 %collective-permute-start = (bf16[2,16,32,128]{3,2,1,0:T(8,128)(2,1)S(1)}, bf16[2,16,32,128]{3,2,1,0:T(8,128)(2,1)S(1)}, u32[]{:S(2)}, u32[]{:S(2)}) collective-permute-start(bf16[2,16,32,128]{3,2,1,0:T(8,128)(2,1)S(1)} %get-tuple-element.19), channel_id=1, source_target_pairs={{0,128},{128,256},{256,384},{1,129},{129,257},{257,385},{2,130},{1... | collective-permute-start | bytes 786440 | tf_op jit(solution)/shard_map/ppermute | solution.py:28
  5.1 10.6 %all-gather.8 = f32[8,2,128]{2,1,0:T(2,128)S(1)} all-gather(f32[1,2,128]{2,1,0:T(2,128)S(1)} %bitcast.16), channel_id=2, replica_groups=mesh['section'=4,'th_0'=4,'th_1'=4,'tw_0'=4,'tw_1'=2] {'tw_0','tw_1'}, dimensions={0}, use_global_device_ids=true | all-gather | bytes 9216 | tf_op jit(solution)/shard_map/all_gather | solution.py:22
  15.7 0.0 copy-start.5
  15.7 0.0 copy-start.6
  15.7 0.0 collective-permute-done.before_ref
  15.8 3.6 %collective-permute-start.1 = (bf16[6,2,32,128]{3,2,1,0:T(8,128)(2,1)S(1)}, bf16[6,2,32,128]{3,2,1,0:T(8,128)(2,1)S(1)}, u32[]{:S(2)}, u32[]{:S(2)}) collective-permute-start(bf16[6,2,32,128]{3,2,1,0:T(8,128)(2,1)S(1)} %pad_maximum_fusion), channel_id=1, source_target_pairs={{0,8},{8,16},{16,24},{24,32},{32,40},{40,48},{48,56},{56,64},{64,7... | collective-permute-start | bytes 294920 | tf_op jit(solution)/shard_map/ppermute | solution.py:28
  19.4 1.3 %collective-permute-start.2 = (bf16[6,2,32,128]{3,2,1,0:T(8,128)(2,1)S(1)}, bf16[6,2,32,128]{3,2,1,0:T(8,128)(2,1)S(1)}, u32[]{:S(2)}, u32[]{:S(2)}) collective-permute-start(bf16[6,2,32,128]{3,2,1,0:T(8,128)(2,1)S(1)} %pad_maximum_fusion.1), channel_id=1, source_target_pairs={{8,0},{16,8},{24,16},{32,24},{40,32},{48,40},{56,48},{64,56},{72,6... | collective-permute-start | bytes 294920 | tf_op jit(solution)/shard_map/ppermute | solution.py:28
  20.8 15.9 %all-gather.9 = f32[4,2,128]{2,1,0:T(2,128)S(1)} all-gather(f32[1,2,128]{2,1,0:T(2,128)S(1)} %bitcast.22), channel_id=3, replica_groups=mesh['section'=4,'th_0'=4,'th_1'=4,'tw_0'=4,'tw_1'=2] {'th_1'}, dimensions={0}, use_global_device_ids=true | all-gather | bytes 5120 | tf_op jit(solution)/shard_map/all_gather | solution.py:22
  36.7 8.6 %all-gather.10 = f32[4,2,128]{2,1,0:T(2,128)S(1)} all-gather(f32[1,2,128]{2,1,0:T(2,128)S(1)} %bitcast.26), channel_id=4, replica_groups=mesh['section'=4,'th_0'=4,'th_1'=4,'tw_0'=4,'tw_1'=2] {'section'}, dimensions={0}, use_global_device_ids=true | all-gather | bytes 5120 | tf_op jit(solution)/shard_map/all_gather | solution.py:22
  45.3 0.0 collective-permute-done.1.above_ref
  45.3 0.0 collective-permute-done.2.below_ref
  45.3 0.1 pad_maximum_fusion.2
  45.5 1.3 %collective-permute-start.3 = (bf16[6,20,2,128]{3,2,1,0:T(2,128)(2,1)S(1)}, bf16[6,20,2,128]{3,2,1,0:T(2,128)(2,1)S(1)}, u32[]{:S(2)}, u32[]{:S(2)}) collective-permute-start(bf16[6,20,2,128]{3,2,1,0:T(2,128)(2,1)S(1)} %pad_maximum_fusion.2), channel_id=1, source_target_pairs={{0,1},{1,2},{2,3},{3,4},{4,5},{5,6},{6,7},{8,9},{9,10},{10,11},{11... | collective-permute-start | bytes 184328 | tf_op jit(solution)/shard_map/ppermute | solution.py:28
  46.8 0.1 pad_maximum_fusion.3
  46.9 1.3 %collective-permute-start.4 = (bf16[6,20,2,128]{3,2,1,0:T(2,128)(2,1)S(1)}, bf16[6,20,2,128]{3,2,1,0:T(2,128)(2,1)S(1)}, u32[]{:S(2)}, u32[]{:S(2)}) collective-permute-start(bf16[6,20,2,128]{3,2,1,0:T(2,128)(2,1)S(1)} %pad_maximum_fusion.3), channel_id=1, source_target_pairs={{1,0},{2,1},{3,2},{4,3},{5,4},{6,5},{7,6},{9,8},{10,9},{11,10},{12... | collective-permute-start | bytes 184328 | tf_op jit(solution)/shard_map/ppermute | solution.py:28
  48.2 16.9 %all-gather.11.sums_ref = f32[4,2,128]{2,1,0:T(2,128)S(1)} all-gather(f32[1,2,128]{2,1,0:T(2,128)S(1)} %bitcast.24), channel_id=5, replica_groups=mesh['section'=4,'th_0'=4,'th_1'=4,'tw_0'=4,'tw_1'=2] {'th_0'}, dimensions={0}, use_global_device_ids=true | all-gather | bytes 5120 | tf_op jit(solution)/shard_map/all_gather | solution.py:245
  65.1 0.0 collective-permute-done.3.left_ref
  65.1 0.0 collective-permute-done.4.right_ref
  65.1 0.0 copy-done.1
  65.1 0.0 copy-done.3
  65.1 0.0 copy-done.4
  65.1 8.3 %first_conv.1 = (f32[18,10,16,128]{3,2,1,0:T(8,128)S(1)}, bf16[18,5,16,128]{3,2,1,0:T(8,128)(2,1)}, f32[2,128]{1,0:T(2,128)S(1)}) custom-call(bf16[4,16,32,128]{3,2,1,0:T(8,128)(2,1)S(1)} %copy-done.1, bf16[2,16,32,128]{3,2,1,0:T(8,128)(2,1)S(1)} %collective-permute-done.before_ref, bf16[6,2,32,128]{3,2,1,0:T(8,128)(2,1)S(1)} %collective-permute-done.1.above_ref, ...), custom_call_target="tpu_custom_call" | custom-call | tf_op jit(solution)/shard_map/first_conv/pallas_call | solution.py:247
  73.5 1.9 %collective-permute-start.5 = (bf16[18,5,16,128]{3,2,1,0:T(8,128)(2,1)}, bf16[18,5,16,128]{3,2,1,0:T(8,128)(2,1)S(1)}, u32[]{:S(2)}, u32[]{:S(2)}) collective-permute-start(bf16[18,5,16,128]{3,2,1,0:T(8,128)(2,1)} %get-tuple-element.31), channel_id=1, source_target_pairs={{0,128},{128,256},{256,384},{1,129},{129,257},{257,385},{2,130},{1... | collective-permute-start | bytes 1105928 | tf_op jit(solution)/shard_map/ppermute | solution.py:28
  75.4 10.4 %all-gather.12 = f32[8,2,128]{2,1,0:T(2,128)S(1)} all-gather(f32[1,2,128]{2,1,0:T(2,128)S(1)} %bitcast.15), channel_id=6, replica_groups=mesh['section'=4,'th_0'=4,'th_1'=4,'tw_0'=4,'tw_1'=2] {'tw_0','tw_1'}, dimensions={0}, use_global_device_ids=true | all-gather | bytes 9216 | tf_op jit(solution)/shard_map/all_gather | solution.py:22
  85.8 8.9 %all-gather.13 = f32[4,2,128]{2,1,0:T(2,128)S(1)} all-gather(f32[1,2,128]{2,1,0:T(2,128)S(1)} %bitcast.23), channel_id=7, replica_groups=mesh['section'=4,'th_0'=4,'th_1'=4,'tw_0'=4,'tw_1'=2] {'th_1'}, dimensions={0}, use_global_device_ids=true | all-gather | bytes 5120 | tf_op jit(solution)/shard_map/all_gather | solution.py:22
  94.7 9.6 %all-gather.14 = f32[4,2,128]{2,1,0:T(2,128)S(1)} all-gather(f32[1,2,128]{2,1,0:T(2,128)S(1)} %bitcast.27), channel_id=8, replica_groups=mesh['section'=4,'th_0'=4,'th_1'=4,'tw_0'=4,'tw_1'=2] {'section'}, dimensions={0}, use_global_device_ids=true | all-gather | bytes 5120 | tf_op jit(solution)/shard_map/all_gather | solution.py:22
  104.3 13.3 %all-gather.15.sums_ref = f32[4,2,128]{2,1,0:T(2,128)S(1)} all-gather(f32[1,2,128]{2,1,0:T(2,128)S(1)} %bitcast.25), channel_id=9, replica_groups=mesh['section'=4,'th_0'=4,'th_1'=4,'tw_0'=4,'tw_1'=2] {'th_0'}, dimensions={0}, use_global_device_ids=true | all-gather | bytes 5120 | tf_op jit(solution)/shard_map/all_gather | solution.py:271
  117.6 0.0 collective-permute-done.5.halo_ref
  117.7 0.0 copy-done.6
  117.7 6.1 %second_conv.1 = bf16[4,16,32,128]{3,2,1,0:T(8,128)(2,1)} custom-call(f32[18,10,16,128]{3,2,1,0:T(8,128)S(1)} %get-tuple-element.30.hidden_ref, bf16[18,5,16,128]{3,2,1,0:T(8,128)(2,1)S(1)} %collective-permute-done.5.halo_ref, f32[4,2,128]{2,1,0:T(2,128)S(1)} %all-gather.15.sums_ref, f32[1,128]{1,0:T(1,128)S(1)} %bitcast.19, f32[1,128]{1,0:T(1,128)S(1)} %bitcast.20, ...), custom_call_target="tpu_custom_call" | custom-call | tf_op jit(solution)/shard_map/second_conv/pallas_call | solution.py:273
  (18 shorter events, 0.2 us)
Async XLA Ops:
  0.0 1.0 copy-start
  1.0 64.1 %copy-start.1 = (bf16[4,16,32,128]{3,2,1,0:T(8,128)(2,1)S(1)}, bf16[4,16,32,128]{3,2,1,0:T(8,128)(2,1)}, u32[]{:S(2)}) copy-start(bf16[4,16,32,128]{3,2,1,0:T(8,128)(2,1)} %feat_ref.5) | copy-start | bytes 1572868
  1.0 64.1 %copy-start.3 = (f32[128]{0:T(128)S(1)}, f32[128]{0:T(128)}, u32[]{:S(2)}) copy-start(f32[128]{0:T(128)} %param.8) | copy-start | bytes 1540
  1.0 64.1 %copy-start.4 = (f32[128]{0:T(128)S(1)}, f32[128]{0:T(128)}, u32[]{:S(2)}) copy-start(f32[128]{0:T(128)} %param.9) | copy-start | bytes 1540
  1.3 14.4 %collective-permute-start = (bf16[2,16,32,128]{3,2,1,0:T(8,128)(2,1)S(1)}, bf16[2,16,32,128]{3,2,1,0:T(8,128)(2,1)S(1)}, u32[]{:S(2)}, u32[]{:S(2)}) collective-permute-start(bf16[2,16,32,128]{3,2,1,0:T(8,128)(2,1)S(1)} %get-tuple-element.19), channel_id=1, source_target_pairs={{0,128},{128,256},{256,384},{1,129},{129,257},{257,385},{2,130},{1... | collective-permute-start | bytes 786440 | tf_op jit(solution)/shard_map/ppermute | solution.py:28
  15.7 101.9 %copy-start.2 = (bf16[3,3,3,128,128]{4,3,2,1,0:T(8,128)(2,1)S(1)}, bf16[3,3,3,128,128]{4,3,2,1,0:T(8,128)(2,1)}, u32[]{:S(2)}) copy-start(bf16[3,3,3,128,128]{4,3,2,1,0:T(8,128)(2,1)} %param.13) | copy-start | bytes 2654212
  15.7 101.9 %copy-start.5 = (f32[128]{0:T(128)S(1)}, f32[128]{0:T(128)}, u32[]{:S(2)}) copy-start(f32[128]{0:T(128)} %param.11) | copy-start | bytes 1540
  15.7 101.9 %copy-start.6 = (f32[128]{0:T(128)S(1)}, f32[128]{0:T(128)}, u32[]{:S(2)}) copy-start(f32[128]{0:T(128)} %param.12) | copy-start | bytes 1540
  15.8 29.5 %collective-permute-start.1 = (bf16[6,2,32,128]{3,2,1,0:T(8,128)(2,1)S(1)}, bf16[6,2,32,128]{3,2,1,0:T(8,128)(2,1)S(1)}, u32[]{:S(2)}, u32[]{:S(2)}) collective-permute-start(bf16[6,2,32,128]{3,2,1,0:T(8,128)(2,1)S(1)} %pad_maximum_fusion), channel_id=1, source_target_pairs={{0,8},{8,16},{16,24},{24,32},{32,40},{40,48},{48,56},{56,64},{64,7... | collective-permute-start | bytes 294920 | tf_op jit(solution)/shard_map/ppermute | solution.py:28
  19.4 25.9 %collective-permute-start.2 = (bf16[6,2,32,128]{3,2,1,0:T(8,128)(2,1)S(1)}, bf16[6,2,32,128]{3,2,1,0:T(8,128)(2,1)S(1)}, u32[]{:S(2)}, u32[]{:S(2)}) collective-permute-start(bf16[6,2,32,128]{3,2,1,0:T(8,128)(2,1)S(1)} %pad_maximum_fusion.1), channel_id=1, source_target_pairs={{8,0},{16,8},{24,16},{32,24},{40,32},{48,40},{56,48},{64,56},{72,6... | collective-permute-start | bytes 294920 | tf_op jit(solution)/shard_map/ppermute | solution.py:28
  45.5 19.7 %collective-permute-start.3 = (bf16[6,20,2,128]{3,2,1,0:T(2,128)(2,1)S(1)}, bf16[6,20,2,128]{3,2,1,0:T(2,128)(2,1)S(1)}, u32[]{:S(2)}, u32[]{:S(2)}) collective-permute-start(bf16[6,20,2,128]{3,2,1,0:T(2,128)(2,1)S(1)} %pad_maximum_fusion.2), channel_id=1, source_target_pairs={{0,1},{1,2},{2,3},{3,4},{4,5},{5,6},{6,7},{8,9},{9,10},{10,11},{11... | collective-permute-start | bytes 184328 | tf_op jit(solution)/shard_map/ppermute | solution.py:28
  46.9 18.3 %collective-permute-start.4 = (bf16[6,20,2,128]{3,2,1,0:T(2,128)(2,1)S(1)}, bf16[6,20,2,128]{3,2,1,0:T(2,128)(2,1)S(1)}, u32[]{:S(2)}, u32[]{:S(2)}) collective-permute-start(bf16[6,20,2,128]{3,2,1,0:T(2,128)(2,1)S(1)} %pad_maximum_fusion.3), channel_id=1, source_target_pairs={{1,0},{2,1},{3,2},{4,3},{5,4},{6,5},{7,6},{9,8},{10,9},{11,10},{12... | collective-permute-start | bytes 184328 | tf_op jit(solution)/shard_map/ppermute | solution.py:28
  73.5 44.2 %collective-permute-start.5 = (bf16[18,5,16,128]{3,2,1,0:T(8,128)(2,1)}, bf16[18,5,16,128]{3,2,1,0:T(8,128)(2,1)S(1)}, u32[]{:S(2)}, u32[]{:S(2)}) collective-permute-start(bf16[18,5,16,128]{3,2,1,0:T(8,128)(2,1)} %get-tuple-element.31), channel_id=1, source_target_pairs={{0,128},{128,256},{256,384},{1,129},{129,257},{257,385},{2,130},{1... | collective-permute-start | bytes 1105928 | tf_op jit(solution)/shard_map/ppermute | solution.py:28

commit v3 on v2

--- a/solution.py
+++ b/solution.py
@@ -26,6 +26,18 @@
     count = lax.axis_size(axis)
     pairs = [(i, i + step) for i in range(count) if 0 <= i + step < count]
     return lax.ppermute(value, axis, pairs)
+
+
+def swapped(toward_next, toward_last, axis, odd):
+    count = lax.axis_size(axis)
+
+    def swap(value, first):
+        pairs = [(i, i + 1) for i in range(first, count - 1, 2)]
+        return lax.ppermute(value, axis, pairs + [(b, a) for a, b in pairs])
+
+    even_first = swap(jnp.where(odd, toward_last, toward_next), 0)
+    odd_first = swap(jnp.where(odd, toward_next, toward_last), 1)
+    return jnp.where(odd, even_first, odd_first), jnp.where(odd, odd_first, even_first)
 
 
 def scale_and_offset(sums_ref, gain_ref, shift_ref, count):
@@ -70,22 +82,42 @@
     return jnp.where(chunk == 0, left_ok, 1.0), jnp.where(chunk == 3, right_ok, 1.0)
 
 
-def conv_block(act_ref, kernel_ref, acc_ref, start, rows, cols):
-    size = rows * cols * 16
-    taps = [(dt, di, dj) for dt in range(3) for di in range(3) for dj in range(3)]
-    step = 2
-    for k in range(0, 27, step):
-        part = taps[k : k + step]
-        lhs = jnp.concatenate(
-            [
-                act_ref[dt, pl.ds(start + di, rows), dj : dj + cols].reshape(size, 128)
-                for dt, di, dj in part
-            ],
-            axis=1,
-        )
-        rhs = kernel_ref[k * 128 : (k + len(part)) * 128, :]
-        new = jnp.dot(lhs, rhs, preferred_element_type=F32)
-        acc_ref[...] = new if k == 0 else acc_ref[...] + new
+def conv_block(act_ref, kernel_ref, pair_ref, single_ref, start, rows, cols):
+    slabs = [(dt, di) for dt in range(3) for di in range(3)]
+
+    def lhs(parts, width):
+        parts = [act_ref[dt, pl.ds(start + di, rows), dj : dj + width] for dt, di, dj in parts]
+        return jnp.concatenate([p.reshape(rows * width * 16, 128) for p in parts], 1)
+
+    def tap(dt, di, dj):
+        k = ((dt * 3 + di) * 3 + dj) * 128
+        return kernel_ref[k : k + 128, :]
+
+    def wide(slab):
+        return jnp.concatenate([tap(*slab, 0), tap(*slab, 1)], 1)
+
+    for k in range(0, 9, 2):
+        first = slabs[k]
+        if k < 8:
+            left = lhs([(*first, 0), (*slabs[k + 1], 0)], cols + 1)
+            right = jnp.concatenate([wide(first), wide(slabs[k + 1])], 0)
+        else:
+            left = lhs([(*first, 0), (*first, 2)], cols + 1)
+            last = tap(*first, 2)
+            last = jnp.concatenate([last, jnp.zeros_like(last)], 1)
+            right = jnp.concatenate([wide(first), last], 0)
+        new = jnp.dot(left, right, preferred_element_type=F32)
+        pair_ref[...] = new if k == 0 else pair_ref[...] + new
+    for k in range(0, 8, 2):
+        left = lhs([(*slabs[k], 2), (*slabs[k + 1], 2)], cols)
+        right = jnp.concatenate([tap(*slabs[k], 2), tap(*slabs[k + 1], 2)], 0)
+        new = jnp.dot(left, right, preferred_element_type=F32)
+        single_ref[...] = new if k == 0 else single_ref[...] + new
+
+
+def clear_last_column(act_ref, rows, column):
+    for h in range(rows):
+        act_ref[2, h, column] = jnp.zeros((16, 128), BF16)
 
 
 def prepare_body(feat_ref, last_ref, top_ref, bottom_ref, head_ref, tail_ref, sums_ref):
@@ -111,7 +143,7 @@
 
 def first_body(count, feat_ref, before_ref, above_ref, below_ref, left_ref, right_ref, sums_ref,
                gain_ref, shift_ref, kernel_ref, hidden_ref, halo_ref, out_sums_ref,
-               flat_ref, act_ref, acc_ref, taps_ref, taps_sem):
+               flat_ref, act_ref, pair_ref, single_ref, taps_ref, taps_sem):
     fetch = pltpu.make_async_copy(kernel_ref, taps_ref, taps_sem)
     fetch.start()
     scale, offset = scale_and_offset(sums_ref, gain_ref, shift_ref, count)
@@ -140,11 +172,15 @@
 
     lax.fori_loop(0, ROWS1 + 2, fill, 0)
 
+    clear_last_column(act_ref, ROWS1 + 2, COLS1 + 2)
     fetch.wait()
 
     def conv(b, _):
-        conv_block(act_ref, taps_ref, acc_ref, b * BLOCK1, BLOCK1, COLS1)
-        hidden_ref[pl.ds(b * BLOCK1, BLOCK1)] = acc_ref[...].reshape(BLOCK1, COLS1, 16, 128)
+        conv_block(act_ref, taps_ref, pair_ref, single_ref, b * BLOCK1, BLOCK1, COLS1)
+        both = pair_ref[...].reshape(BLOCK1, COLS1 + 1, 16, 256)
+        total = both[:, :COLS1, :, :128] + both[:, 1:, :, 128:]
+        total += single_ref[...].reshape(BLOCK1, COLS1, 16, 128)
+        hidden_ref[pl.ds(b * BLOCK1, BLOCK1)] = total
         return 0
 
     lax.fori_loop(0, ROWS1 // BLOCK1, conv, 0)
@@ -168,7 +204,7 @@
 
 
 def second_body(count, hidden_ref, halo_ref, sums_ref, gain_ref, shift_ref, kernel_ref, feat_ref,
-                out_ref, act_ref, acc_ref, flat_ref):
+                out_ref, act_ref, pair_ref, single_ref, flat_ref):
     scale, offset = scale_and_offset(sums_ref, gain_ref, shift_ref, count)
     before_ok, above_ok, below_ok, left_ok, right_ok = edges()
     left_mask, right_mask = column_masks(left_ok, right_ok)
@@ -185,13 +221,18 @@
 
     lax.fori_loop(0, ROWS2 + 2, fill, 0)
 
+    clear_last_column(act_ref, ROWS2 + 2, COLS2 + 2)
+
     def conv(b, _):
-        conv_block(act_ref, kernel_ref, acc_ref, b * BLOCK2, BLOCK2, COLS2)
+        conv_block(act_ref, kernel_ref, pair_ref, single_ref, b * BLOCK2, BLOCK2, COLS2)
 
         def spread(i, _):
             h = b * BLOCK2 + i
             for m in range(COLS2):
-                tile = acc_ref[pl.ds(pl.multiple_of((i * COLS2 + m) * 16, 16), 16), :]
+                at = pl.multiple_of((i * (COLS2 + 1) + m) * 16, 16)
+                tile = pair_ref[pl.ds(at, 16), :128] + pair_ref[pl.ds(at + 16, 16), 128:]
+                at = pl.multiple_of((i * COLS2 + m) * 16, 16)
+                tile += single_ref[pl.ds(at, 16), :]
                 for t in range(4):
                     flat_ref[t, pl.ds(m, 4, stride=8), :] = tile[4 * t : 4 * t + 4]
             for t in range(4):
@@ -230,8 +271,12 @@
     before = shifted(last, "section", 1)
     sums = gathered_sum(sums, TW)
     before, sums = lax.optimization_barrier((before, sums))
-    above = shifted(jnp.concatenate([before[:, -2:], bottom], 0), TH, 1)
-    below = shifted(jnp.concatenate([before[:, :2], top], 0), TH, -1)
+    above, below = swapped(
+        jnp.concatenate([before[:, -2:], bottom], 0),
+        jnp.concatenate([before[:, :2], top], 0),
+        TH,
+        (lax.axis_index("th_1") & 1) == 1,
+    )
     sums = gathered_sum(sums, "th_1")
     sums = gathered_sum(sums, "section")
     above, below, sums = lax.optimization_barrier((above, below, sums))
@@ -240,22 +285,27 @@
         own = jnp.concatenate([before[:, :, s], own], 0)
         return jnp.concatenate([above[:, :, s], own, below[:, :, s]], 1)
 
-    left = shifted(columns(tail, slice(-2, None)), TW, 1)
-    right = shifted(columns(head, slice(0, 2)), TW, -1)
+    left, right = swapped(
+        columns(tail, slice(-2, None)),
+        columns(head, slice(0, 2)),
+        TW,
+        lax.axis_index("tw_1") == 1,
+    )
     sums = lax.all_gather(sums, "th_0")
 
     hidden, halo, sums = pl.pallas_call(
         functools.partial(first_body, count),
         out_shape=(
             jax.ShapeDtypeStruct((ROWS1, COLS1, 16, 128), F32),
-            jax.ShapeDtypeStruct((ROWS1, COLS1 // 2, 16, 128), BF16),
+            pltpu.VMEM((ROWS1, COLS1 // 2, 16, 128), BF16),
             jax.ShapeDtypeStruct((2, 128), F32),
         ),
         in_specs=[*in_vmem(9), pl.BlockSpec(memory_space=pltpu.HBM)],
         out_specs=tuple(in_vmem(3)),
         scratch_shapes=[
             pltpu.VMEM((6, 20, 48, 128), F32),
-            pltpu.VMEM((3, ROWS1 + 2, COLS1 + 2, 16, 128), BF16),
+            pltpu.VMEM((3, ROWS1 + 2, COLS1 + 3, 16, 128), BF16),
+            pltpu.VMEM((BLOCK1 * (COLS1 + 1) * 16, 256), F32),
             pltpu.VMEM((BLOCK1 * COLS1 * 16, 128), F32),
             pltpu.VMEM((27 * 128, 128), BF16),
             pltpu.SemaphoreType.DMA,
@@ -276,7 +326,8 @@
         in_specs=in_vmem(7),
         out_specs=in_vmem(1)[0],
         scratch_shapes=[
-            pltpu.VMEM((3, ROWS2 + 2, COLS2 + 2, 16, 128), BF16),
+            pltpu.VMEM((3, ROWS2 + 2, COLS2 + 3, 16, 128), BF16),
+            pltpu.VMEM((BLOCK2 * (COLS2 + 1) * 16, 256), F32),
             pltpu.VMEM((BLOCK2 * COLS2 * 16, 128), F32),
             pltpu.VMEM((4, 32, 128), F32),
         ],

time: 124 us -> 118 us (0.952)
  blocking collectives: 94.2 us -> 88.5 us
  Pallas kernels: 14.6 us -> 12.3 us
  starting transfers between devices: 13.2 us -> 15.3 us
    ppermute x0 -> x4, starting transfers between devices: none -> 9.55 us  [swap(): return lax.ppermute(value, axis, pairs + [(b, a) for a, b in pairs])]
    ppermute x6 -> x2, starting transfers between devices: 13.2 us -> 5.74 us  [shifted(): return lax.ppermute(value, axis, pairs)]
    all_gather x6, blocking collectives: 64 us -> 60.6 us  [gathered_sum(): return jnp.sum(lax.all_gather(value, axis), axis=0)]
    all_gather x2, blocking collectives: 30.3 us -> 27.9 us  [shards(): sums = lax.all_gather(sums, 'th_0')]
    pallas_call x1, Pallas kernels: 8.32 us -> 6.87 us  [shards(): pl.pallas_call(functools.partial(first_body, count), out_shape=(jax.Shape...]
where the time goes in v3:
time: 118 us
  blocking collectives  88.5 us (75%)
  starting transfers between devices  15.3 us (13%)
  Pallas kernels  12.3 us (10%)
    all_gather x6, blocking collectives, gathered_sum(): return jnp.sum(lax.all_gather(value, axis), axis=0)  60.6 us
    all_gather x2, blocking collectives, shards(): sums = lax.all_gather(sums, 'th_0')  27.9 us
    ppermute x4, starting transfers between devices, swap(): return lax.ppermute(value, axis, pairs + [(b, a) for a, b in pairs])  9.55 us
    pallas_call x1, Pallas kernels, shards(): pl.pallas_call(functools.partial(first_body, count), out_shape=(jax.Shape...  6.87 us
    ppermute x2, starting transfers between devices, shifted(): return lax.ppermute(value, axis, pairs)  5.74 us
    pallas_call x1, Pallas kernels, shards(): pl.pallas_call(functools.partial(second_body, count), out_shape=jax.Shape...  5.24 us
  transfers between devices with their start and end apart: 6, of which 0 were waited for; matrix products, arithmetic and copies ran while one was open for 0% of the time, Pallas kernels for 0%

profile of v3, /device:TPU:32, one launch (start us, length us, event | category | flops | bytes accessed | tf_op | source)
XLA Modules:
  0.0 117.9 jit_solution(15733570319353607897)
XLA Ops:
  0.0 1.0 copy-done
  1.0 0.2 prepare.1
  1.3 3.8 %collective-permute-start = (bf16[2,16,32,128]{3,2,1,0:T(8,128)(2,1)S(1)}, bf16[2,16,32,128]{3,2,1,0:T(8,128)(2,1)S(1)}, u32[]{:S(2)}, u32[]{:S(2)}) collective-permute-start(bf16[2,16,32,128]{3,2,1,0:T(8,128)(2,1)S(1)} %get-tuple-element.19), channel_id=1, source_target_pairs={{0,128},{128,256},{256,384},{1,129},{129,257},{257,385},{2,130},{1... | collective-permute-start | bytes 786440 | tf_op jit(solution)/shard_map/ppermute | solution.py:28
  5.1 10.6 %all-gather.8 = f32[8,2,128]{2,1,0:T(2,128)S(1)} all-gather(f32[1,2,128]{2,1,0:T(2,128)S(1)} %bitcast.24), channel_id=2, replica_groups=mesh['section'=4,'th_0'=4,'th_1'=4,'tw_0'=4,'tw_1'=2] {'tw_0','tw_1'}, dimensions={0}, use_global_device_ids=true | all-gather | bytes 9216 | tf_op jit(solution)/shard_map/all_gather | solution.py:22
  15.7 0.0 collective-permute-done.before_ref
  15.8 0.7 collective-permute-start.2
  16.4 6.3 %collective-permute-start.1 = (bf16[6,2,32,128]{3,2,1,0:T(8,128)(2,1)S(1)}, bf16[6,2,32,128]{3,2,1,0:T(8,128)(2,1)S(1)}, u32[]{:S(2)}, u32[]{:S(2)}) collective-permute-start(bf16[6,2,32,128]{3,2,1,0:T(8,128)(2,1)S(1)} %get-tuple-element.43), channel_id=1, source_target_pairs={{0,8},{16,24},{32,40},{48,56},{64,72},{80,88},{96,104},{112,120},{... | collective-permute-start | bytes 294920 | tf_op jit(solution)/shard_map/ppermute | solution.py:36
  22.8 13.8 %all-gather.9 = f32[4,2,128]{2,1,0:T(2,128)S(1)} all-gather(f32[1,2,128]{2,1,0:T(2,128)S(1)} %bitcast.36), channel_id=3, replica_groups=mesh['section'=4,'th_0'=4,'th_1'=4,'tw_0'=4,'tw_1'=2] {'th_1'}, dimensions={0}, use_global_device_ids=true | all-gather | bytes 5120 | tf_op jit(solution)/shard_map/all_gather | solution.py:22
  36.6 8.5 %all-gather.10 = f32[4,2,128]{2,1,0:T(2,128)S(1)} all-gather(f32[1,2,128]{2,1,0:T(2,128)S(1)} %bitcast.40), channel_id=4, replica_groups=mesh['section'=4,'th_0'=4,'th_1'=4,'tw_0'=4,'tw_1'=2] {'section'}, dimensions={0}, use_global_device_ids=true | all-gather | bytes 5120 | tf_op jit(solution)/shard_map/all_gather | solution.py:22
  45.1 0.0 collective-permute-done.2
  45.1 0.0 collective-permute-done.1
  45.1 0.0 copy-start.2
  45.1 0.0 copy-start.5
  45.1 0.0 copy-start.6
  45.2 0.2 broadcast_select_fusion.2
  45.4 1.9 %collective-permute-start.3 = (bf16[6,20,2,128]{3,2,1,0:T(2,128)(2,1)S(1)}, bf16[6,20,2,128]{3,2,1,0:T(2,128)(2,1)S(1)}, u32[]{:S(2)}, u32[]{:S(2)}) collective-permute-start(bf16[6,20,2,128]{3,2,1,0:T(2,128)(2,1)S(1)} %bitcast.33), channel_id=1, source_target_pairs={{0,1},{2,3},{4,5},{6,7},{1,0},{3,2},{5,4},{7,6},{8,9},{10,11},{12,... | collective-permute-start | bytes 184328 | tf_op jit(solution)/shard_map/ppermute | solution.py:36
  47.4 0.7 collective-permute-start.4
  48.0 17.0 %all-gather.11.sums_ref = f32[4,2,128]{2,1,0:T(2,128)S(1)} all-gather(f32[1,2,128]{2,1,0:T(2,128)S(1)} %bitcast.38), channel_id=5, replica_groups=mesh['section'=4,'th_0'=4,'th_1'=4,'tw_0'=4,'tw_1'=2] {'th_0'}, dimensions={0}, use_global_device_ids=true | all-gather | bytes 5120 | tf_op jit(solution)/shard_map/all_gather | solution.py:294
  65.0 0.0 collective-permute-done.3
  65.0 0.0 collective-permute-done.4
  65.0 0.0 copy-done.1
  65.1 0.0 copy-done.3
  65.1 0.0 copy-done.4
  65.1 6.9 %first_conv.1 = (f32[18,10,16,128]{3,2,1,0:T(8,128)S(1)}, bf16[18,5,16,128]{3,2,1,0:T(8,128)(2,1)}, f32[2,128]{1,0:T(2,128)S(1)}) custom-call(bf16[4,16,32,128]{3,2,1,0:T(8,128)(2,1)S(1)} %copy-done.1, bf16[2,16,32,128]{3,2,1,0:T(8,128)(2,1)S(1)} %collective-permute-done.before_ref, bf16[6,2,32,128]{3,2,1,0:T(8,128)(2,1)S(1)} %get-tuple-element.25.above_ref, ...), custom_call_target="tpu_custom_call" | custom-call | tf_op jit(solution)/shard_map/first_conv/pallas_call | solution.py:296
  71.9 1.9 %collective-permute-start.5 = (bf16[18,5,16,128]{3,2,1,0:T(8,128)(2,1)}, bf16[18,5,16,128]{3,2,1,0:T(8,128)(2,1)S(1)}, u32[]{:S(2)}, u32[]{:S(2)}) collective-permute-start(bf16[18,5,16,128]{3,2,1,0:T(8,128)(2,1)} %get-tuple-element.31), channel_id=1, source_target_pairs={{0,128},{128,256},{256,384},{1,129},{129,257},{257,385},{2,130},{1... | collective-permute-start | bytes 1105928 | tf_op jit(solution)/shard_map/ppermute | solution.py:28
  73.9 11.2 %all-gather.12 = f32[8,2,128]{2,1,0:T(2,128)S(1)} all-gather(f32[1,2,128]{2,1,0:T(2,128)S(1)} %bitcast.25), channel_id=6, replica_groups=mesh['section'=4,'th_0'=4,'th_1'=4,'tw_0'=4,'tw_1'=2] {'tw_0','tw_1'}, dimensions={0}, use_global_device_ids=true | all-gather | bytes 9216 | tf_op jit(solution)/shard_map/all_gather | solution.py:22
  85.1 7.0 %all-gather.13 = f32[4,2,128]{2,1,0:T(2,128)S(1)} all-gather(f32[1,2,128]{2,1,0:T(2,128)S(1)} %bitcast.37), channel_id=7, replica_groups=mesh['section'=4,'th_0'=4,'th_1'=4,'tw_0'=4,'tw_1'=2] {'th_1'}, dimensions={0}, use_global_device_ids=true | all-gather | bytes 5120 | tf_op jit(solution)/shard_map/all_gather | solution.py:22
  92.1 9.6 %all-gather.14 = f32[4,2,128]{2,1,0:T(2,128)S(1)} all-gather(f32[1,2,128]{2,1,0:T(2,128)S(1)} %bitcast.41), channel_id=8, replica_groups=mesh['section'=4,'th_0'=4,'th_1'=4,'tw_0'=4,'tw_1'=2] {'section'}, dimensions={0}, use_global_device_ids=true | all-gather | bytes 5120 | tf_op jit(solution)/shard_map/all_gather | solution.py:22
  101.7 10.9 %all-gather.15.sums_ref = f32[4,2,128]{2,1,0:T(2,128)S(1)} all-gather(f32[1,2,128]{2,1,0:T(2,128)S(1)} %bitcast.39), channel_id=9, replica_groups=mesh['section'=4,'th_0'=4,'th_1'=4,'tw_0'=4,'tw_1'=2] {'th_0'}, dimensions={0}, use_global_device_ids=true | all-gather | bytes 5120 | tf_op jit(solution)/shard_map/all_gather | solution.py:321
  112.6 0.0 collective-permute-done.5.halo_ref
  112.6 0.0 copy-done.2
  112.6 5.2 %second_conv.1 = bf16[4,16,32,128]{3,2,1,0:T(8,128)(2,1)} custom-call(f32[18,10,16,128]{3,2,1,0:T(8,128)S(1)} %get-tuple-element.30.hidden_ref, bf16[18,5,16,128]{3,2,1,0:T(8,128)(2,1)S(1)} %collective-permute-done.5.halo_ref, f32[4,2,128]{2,1,0:T(2,128)S(1)} %all-gather.15.sums_ref, f32[1,128]{1,0:T(1,128)S(1)} %bitcast.28, f32[1,128]{1,0:T(1,128)S(1)} %bitcast.29, ...), custom_call_target="tpu_custom_call" | custom-call | tf_op jit(solution)/shard_map/second_conv/pallas_call | solution.py:323
  (19 shorter events, 0.2 us)
Async XLA Ops:
  0.0 1.0 copy-start
  1.0 64.0 %copy-start.1 = (bf16[4,16,32,128]{3,2,1,0:T(8,128)(2,1)S(1)}, bf16[4,16,32,128]{3,2,1,0:T(8,128)(2,1)}, u32[]{:S(2)}) copy-start(bf16[4,16,32,128]{3,2,1,0:T(8,128)(2,1)} %feat_ref.5) | copy-start | bytes 1572868
  1.0 64.0 %copy-start.3 = (f32[128]{0:T(128)S(1)}, f32[128]{0:T(128)}, u32[]{:S(2)}) copy-start(f32[128]{0:T(128)} %param.8) | copy-start | bytes 1540
  1.0 64.0 %copy-start.4 = (f32[128]{0:T(128)S(1)}, f32[128]{0:T(128)}, u32[]{:S(2)}) copy-start(f32[128]{0:T(128)} %param.9) | copy-start | bytes 1540
  1.3 14.4 %collective-permute-start = (bf16[2,16,32,128]{3,2,1,0:T(8,128)(2,1)S(1)}, bf16[2,16,32,128]{3,2,1,0:T(8,128)(2,1)S(1)}, u32[]{:S(2)}, u32[]{:S(2)}) collective-permute-start(bf16[2,16,32,128]{3,2,1,0:T(8,128)(2,1)S(1)} %get-tuple-element.19), channel_id=1, source_target_pairs={{0,128},{128,256},{256,384},{1,129},{129,257},{257,385},{2,130},{1... | collective-permute-start | bytes 786440 | tf_op jit(solution)/shard_map/ppermute | solution.py:28
  15.8 29.3 %collective-permute-start.2 = (bf16[6,2,32,128]{3,2,1,0:T(8,128)(2,1)S(1)}, bf16[6,2,32,128]{3,2,1,0:T(8,128)(2,1)S(1)}, u32[]{:S(2)}, u32[]{:S(2)}) collective-permute-start(bf16[6,2,32,128]{3,2,1,0:T(8,128)(2,1)S(1)} %get-tuple-element.42), channel_id=1, source_target_pairs={{8,16},{24,32},{40,48},{56,64},{72,80},{88,96},{104,112},{16,8},{3... | collective-permute-start | bytes 294920 | tf_op jit(solution)/shard_map/ppermute | solution.py:36
  16.4 28.7 %collective-permute-start.1 = (bf16[6,2,32,128]{3,2,1,0:T(8,128)(2,1)S(1)}, bf16[6,2,32,128]{3,2,1,0:T(8,128)(2,1)S(1)}, u32[]{:S(2)}, u32[]{:S(2)}) collective-permute-start(bf16[6,2,32,128]{3,2,1,0:T(8,128)(2,1)S(1)} %get-tuple-element.43), channel_id=1, source_target_pairs={{0,8},{16,24},{32,40},{48,56},{64,72},{80,88},{96,104},{112,120},{... | collective-permute-start | bytes 294920 | tf_op jit(solution)/shard_map/ppermute | solution.py:36
  45.1 67.5 %copy-start.2 = (bf16[3,3,3,128,128]{4,3,2,1,0:T(8,128)(2,1)S(1)}, bf16[3,3,3,128,128]{4,3,2,1,0:T(8,128)(2,1)}, u32[]{:S(2)}) copy-start(bf16[3,3,3,128,128]{4,3,2,1,0:T(8,128)(2,1)} %param.13) | copy-start | bytes 2654212
  45.1 67.5 %copy-start.5 = (f32[128]{0:T(128)S(1)}, f32[128]{0:T(128)}, u32[]{:S(2)}) copy-start(f32[128]{0:T(128)} %param.11) | copy-start | bytes 1540
  45.1 67.5 %copy-start.6 = (f32[128]{0:T(128)S(1)}, f32[128]{0:T(128)}, u32[]{:S(2)}) copy-start(f32[128]{0:T(128)} %param.12) | copy-start | bytes 1540
  45.4 19.6 %collective-permute-start.3 = (bf16[6,20,2,128]{3,2,1,0:T(2,128)(2,1)S(1)}, bf16[6,20,2,128]{3,2,1,0:T(2,128)(2,1)S(1)}, u32[]{:S(2)}, u32[]{:S(2)}) collective-permute-start(bf16[6,20,2,128]{3,2,1,0:T(2,128)(2,1)S(1)} %bitcast.33), channel_id=1, source_target_pairs={{0,1},{2,3},{4,5},{6,7},{1,0},{3,2},{5,4},{7,6},{8,9},{10,11},{12,... | collective-permute-start | bytes 184328 | tf_op jit(solution)/shard_map/ppermute | solution.py:36
  47.4 17.6 %collective-permute-start.4 = (bf16[6,20,2,128]{3,2,1,0:T(2,128)(2,1)S(1)}, bf16[6,20,2,128]{3,2,1,0:T(2,128)(2,1)S(1)}, u32[]{:S(2)}, u32[]{:S(2)}) collective-permute-start(bf16[6,20,2,128]{3,2,1,0:T(2,128)(2,1)S(1)} %get-tuple-element.33), channel_id=1, source_target_pairs={{1,2},{3,4},{5,6},{2,1},{4,3},{6,5},{9,10},{11,12},{13,14},{10,9},... | collective-permute-start | bytes 184328 | tf_op jit(solution)/shard_map/ppermute | solution.py:36
  71.9 40.7 %collective-permute-start.5 = (bf16[18,5,16,128]{3,2,1,0:T(8,128)(2,1)}, bf16[18,5,16,128]{3,2,1,0:T(8,128)(2,1)S(1)}, u32[]{:S(2)}, u32[]{:S(2)}) collective-permute-start(bf16[18,5,16,128]{3,2,1,0:T(8,128)(2,1)} %get-tuple-element.31), channel_id=1, source_target_pairs={{0,128},{128,256},{256,384},{1,129},{129,257},{257,385},{2,130},{1... | collective-permute-start | bytes 1105928 | tf_op jit(solution)/shard_map/ppermute | solution.py:28

commit v4 on v3

--- a/solution.py
+++ b/solution.py
@@ -82,12 +82,12 @@
     return jnp.where(chunk == 0, left_ok, 1.0), jnp.where(chunk == 3, right_ok, 1.0)
 
 
-def conv_block(act_ref, kernel_ref, pair_ref, single_ref, start, rows, cols):
+def conv_block(act_ref, kernel_ref, pair_ref, rows_ref, single_ref, start, rows, cols):
     slabs = [(dt, di) for dt in range(3) for di in range(3)]
 
-    def lhs(parts, width):
-        parts = [act_ref[dt, pl.ds(start + di, rows), dj : dj + width] for dt, di, dj in parts]
-        return jnp.concatenate([p.reshape(rows * width * 16, 128) for p in parts], 1)
+    def lhs(parts, width, height=rows):
+        parts = [act_ref[dt, pl.ds(start + di, height), dj : dj + width] for dt, di, dj in parts]
+        return jnp.concatenate([p.reshape(height * width * 16, 128) for p in parts], 1)
 
     def tap(dt, di, dj):
         k = ((dt * 3 + di) * 3 + dj) * 128
@@ -108,11 +108,16 @@
             right = jnp.concatenate([wide(first), last], 0)
         new = jnp.dot(left, right, preferred_element_type=F32)
         pair_ref[...] = new if k == 0 else pair_ref[...] + new
-    for k in range(0, 8, 2):
-        left = lhs([(*slabs[k], 2), (*slabs[k + 1], 2)], cols)
-        right = jnp.concatenate([tap(*slabs[k], 2), tap(*slabs[k + 1], 2)], 0)
+    for k, frames in enumerate(((0, 1), (2,))):
+        left = lhs([(dt, 0, 2) for dt in frames], cols, rows + 1)
+        right = jnp.concatenate(
+            [jnp.concatenate([tap(dt, 0, 2), tap(dt, 1, 2)], 1) for dt in frames], 0
+        )
         new = jnp.dot(left, right, preferred_element_type=F32)
-        single_ref[...] = new if k == 0 else single_ref[...] + new
+        rows_ref[...] = new if k == 0 else rows_ref[...] + new
+    left = lhs([(0, 2, 2), (1, 2, 2)], cols)
+    right = jnp.concatenate([tap(0, 2, 2), tap(1, 2, 2)], 0)
+    single_ref[...] = jnp.dot(left, right, preferred_element_type=F32)
 
 
 def clear_last_column(act_ref, rows, column):
@@ -137,13 +142,13 @@
     sums_ref[1:2, :] = jnp.sum(second, 0, keepdims=True)
 
 
-ROWS1, COLS1, BLOCK1 = 18, CHUNK + 2, 6
-ROWS2, COLS2, BLOCK2 = 16, CHUNK, 8
+ROWS1, COLS1, BLOCK1 = 18, CHUNK + 2, 18
+ROWS2, COLS2, BLOCK2 = 16, CHUNK, 16
 
 
 def first_body(count, feat_ref, before_ref, above_ref, below_ref, left_ref, right_ref, sums_ref,
                gain_ref, shift_ref, kernel_ref, hidden_ref, halo_ref, out_sums_ref,
-               flat_ref, act_ref, pair_ref, single_ref, taps_ref, taps_sem):
+               flat_ref, act_ref, pair_ref, rows_ref, single_ref, taps_ref, taps_sem):
     fetch = pltpu.make_async_copy(kernel_ref, taps_ref, taps_sem)
     fetch.start()
     scale, offset = scale_and_offset(sums_ref, gain_ref, shift_ref, count)
@@ -176,9 +181,11 @@
     fetch.wait()
 
     def conv(b, _):
-        conv_block(act_ref, taps_ref, pair_ref, single_ref, b * BLOCK1, BLOCK1, COLS1)
+        conv_block(act_ref, taps_ref, pair_ref, rows_ref, single_ref, b * BLOCK1, BLOCK1, COLS1)
         both = pair_ref[...].reshape(BLOCK1, COLS1 + 1, 16, 256)
         total = both[:, :COLS1, :, :128] + both[:, 1:, :, 128:]
+        both = rows_ref[...].reshape(BLOCK1 + 1, COLS1, 16, 256)
+        total += both[:BLOCK1, :, :, :128] + both[1:, :, :, 128:]
         total += single_ref[...].reshape(BLOCK1, COLS1, 16, 128)
         hidden_ref[pl.ds(b * BLOCK1, BLOCK1)] = total
         return 0
@@ -204,7 +211,7 @@
 
 
 def second_body(count, hidden_ref, halo_ref, sums_ref, gain_ref, shift_ref, kernel_ref, feat_ref,
-                out_ref, act_ref, pair_ref, single_ref, flat_ref):
+                out_ref, act_ref, pair_ref, rows_ref, single_ref, flat_ref):
     scale, offset = scale_and_offset(sums_ref, gain_ref, shift_ref, count)
     before_ok, above_ok, below_ok, left_ok, right_ok = edges()
     left_mask, right_mask = column_masks(left_ok, right_ok)
@@ -224,7 +231,7 @@
     clear_last_column(act_ref, ROWS2 + 2, COLS2 + 2)
 
     def conv(b, _):
-        conv_block(act_ref, kernel_ref, pair_ref, single_ref, b * BLOCK2, BLOCK2, COLS2)
+        conv_block(act_ref, kernel_ref, pair_ref, rows_ref, single_ref, b * BLOCK2, BLOCK2, COLS2)
 
         def spread(i, _):
             h = b * BLOCK2 + i
@@ -232,6 +239,8 @@
                 at = pl.multiple_of((i * (COLS2 + 1) + m) * 16, 16)
                 tile = pair_ref[pl.ds(at, 16), :128] + pair_ref[pl.ds(at + 16, 16), 128:]
                 at = pl.multiple_of((i * COLS2 + m) * 16, 16)
+                below = pl.multiple_of(((i + 1) * COLS2 + m) * 16, 16)
+                tile += rows_ref[pl.ds(at, 16), :128] + rows_ref[pl.ds(below, 16), 128:]
                 tile += single_ref[pl.ds(at, 16), :]
                 for t in range(4):
                     flat_ref[t, pl.ds(m, 4, stride=8), :] = tile[4 * t : 4 * t + 4]
@@ -306,6 +315,7 @@
             pltpu.VMEM((6, 20, 48, 128), F32),
             pltpu.VMEM((3, ROWS1 + 2, COLS1 + 3, 16, 128), BF16),
             pltpu.VMEM((BLOCK1 * (COLS1 + 1) * 16, 256), F32),
+            pltpu.VMEM(((BLOCK1 + 1) * COLS1 * 16, 256), F32),
             pltpu.VMEM((BLOCK1 * COLS1 * 16, 128), F32),
             pltpu.VMEM((27 * 128, 128), BF16),
             pltpu.SemaphoreType.DMA,
@@ -328,6 +338,7 @@
         scratch_shapes=[
             pltpu.VMEM((3, ROWS2 + 2, COLS2 + 3, 16, 128), BF16),
             pltpu.VMEM((BLOCK2 * (COLS2 + 1) * 16, 256), F32),
+            pltpu.VMEM(((BLOCK2 + 1) * COLS2 * 16, 256), F32),
             pltpu.VMEM((BLOCK2 * COLS2 * 16, 128), F32),
             pltpu.VMEM((4, 32, 128), F32),
         ],

time: 118 us -> 117 us (level)
  no operation moved by 1% of the time
where the time goes in v4:
time: 117 us
  blocking collectives  88.5 us (76%)
  starting transfers between devices  15.3 us (13%)
  Pallas kernels  11.5 us (10%)
    all_gather x6, blocking collectives, gathered_sum(): return jnp.sum(lax.all_gather(value, axis), axis=0)  60.6 us
    all_gather x2, blocking collectives, shards(): sums = lax.all_gather(sums, 'th_0')  27.9 us
    ppermute x4, starting transfers between devices, swap(): return lax.ppermute(value, axis, pairs + [(b, a) for a, b in pairs])  9.55 us
    pallas_call x1, Pallas kernels, shards(): pl.pallas_call(functools.partial(first_body, count), out_shape=(jax.Shape...  6.18 us
    ppermute x2, starting transfers between devices, shifted(): return lax.ppermute(value, axis, pairs)  5.74 us
    pallas_call x1, Pallas kernels, shards(): pl.pallas_call(functools.partial(second_body, count), out_shape=jax.Shape...  5.07 us
  transfers between devices with their start and end apart: 6, of which 0 were waited for; matrix products, arithmetic and copies ran while one was open for 0% of the time, Pallas kernels for 0%

profile of v4, /device:TPU:32, one launch (start us, length us, event | category | flops | bytes accessed | tf_op | source)
XLA Modules:
  0.0 117.0 jit_solution(8746192685012063521)
XLA Ops:
  0.0 1.0 copy-done
  1.0 0.2 prepare.1
  1.3 3.8 %collective-permute-start = (bf16[2,16,32,128]{3,2,1,0:T(8,128)(2,1)S(1)}, bf16[2,16,32,128]{3,2,1,0:T(8,128)(2,1)S(1)}, u32[]{:S(2)}, u32[]{:S(2)}) collective-permute-start(bf16[2,16,32,128]{3,2,1,0:T(8,128)(2,1)S(1)} %get-tuple-element.19), channel_id=1, source_target_pairs={{0,128},{128,256},{256,384},{1,129},{129,257},{257,385},{2,130},{1... | collective-permute-start | bytes 786440 | tf_op jit(solution)/shard_map/ppermute | solution.py:28
  5.1 10.6 %all-gather.8 = f32[8,2,128]{2,1,0:T(2,128)S(1)} all-gather(f32[1,2,128]{2,1,0:T(2,128)S(1)} %bitcast.24), channel_id=2, replica_groups=mesh['section'=4,'th_0'=4,'th_1'=4,'tw_0'=4,'tw_1'=2] {'tw_0','tw_1'}, dimensions={0}, use_global_device_ids=true | all-gather | bytes 9216 | tf_op jit(solution)/shard_map/all_gather | solution.py:22
  15.7 0.0 collective-permute-done.before_ref
  15.8 0.7 collective-permute-start.2
  16.4 6.3 %collective-permute-start.1 = (bf16[6,2,32,128]{3,2,1,0:T(8,128)(2,1)S(1)}, bf16[6,2,32,128]{3,2,1,0:T(8,128)(2,1)S(1)}, u32[]{:S(2)}, u32[]{:S(2)}) collective-permute-start(bf16[6,2,32,128]{3,2,1,0:T(8,128)(2,1)S(1)} %get-tuple-element.43), channel_id=1, source_target_pairs={{0,8},{16,24},{32,40},{48,56},{64,72},{80,88},{96,104},{112,120},{... | collective-permute-start | bytes 294920 | tf_op jit(solution)/shard_map/ppermute | solution.py:36
  22.8 13.8 %all-gather.9 = f32[4,2,128]{2,1,0:T(2,128)S(1)} all-gather(f32[1,2,128]{2,1,0:T(2,128)S(1)} %bitcast.36), channel_id=3, replica_groups=mesh['section'=4,'th_0'=4,'th_1'=4,'tw_0'=4,'tw_1'=2] {'th_1'}, dimensions={0}, use_global_device_ids=true | all-gather | bytes 5120 | tf_op jit(solution)/shard_map/all_gather | solution.py:22
  36.6 8.5 %all-gather.10 = f32[4,2,128]{2,1,0:T(2,128)S(1)} all-gather(f32[1,2,128]{2,1,0:T(2,128)S(1)} %bitcast.40), channel_id=4, replica_groups=mesh['section'=4,'th_0'=4,'th_1'=4,'tw_0'=4,'tw_1'=2] {'section'}, dimensions={0}, use_global_device_ids=true | all-gather | bytes 5120 | tf_op jit(solution)/shard_map/all_gather | solution.py:22
  45.1 0.0 collective-permute-done.2
  45.1 0.0 collective-permute-done.1
  45.1 0.0 copy-start.2
  45.1 0.0 copy-start.5
  45.1 0.0 copy-start.6
  45.2 0.2 broadcast_select_fusion.2
  45.4 1.9 %collective-permute-start.3 = (bf16[6,20,2,128]{3,2,1,0:T(2,128)(2,1)S(1)}, bf16[6,20,2,128]{3,2,1,0:T(2,128)(2,1)S(1)}, u32[]{:S(2)}, u32[]{:S(2)}) collective-permute-start(bf16[6,20,2,128]{3,2,1,0:T(2,128)(2,1)S(1)} %bitcast.33), channel_id=1, source_target_pairs={{0,1},{2,3},{4,5},{6,7},{1,0},{3,2},{5,4},{7,6},{8,9},{10,11},{12,... | collective-permute-start | bytes 184328 | tf_op jit(solution)/shard_map/ppermute | solution.py:36
  47.4 0.7 collective-permute-start.4
  48.0 17.0 %all-gather.11.sums_ref = f32[4,2,128]{2,1,0:T(2,128)S(1)} all-gather(f32[1,2,128]{2,1,0:T(2,128)S(1)} %bitcast.38), channel_id=5, replica_groups=mesh['section'=4,'th_0'=4,'th_1'=4,'tw_0'=4,'tw_1'=2] {'th_0'}, dimensions={0}, use_global_device_ids=true | all-gather | bytes 5120 | tf_op jit(solution)/shard_map/all_gather | solution.py:303
  65.0 0.0 collective-permute-done.3
  65.0 0.0 collective-permute-done.4
  65.0 0.0 copy-done.1
  65.1 0.0 copy-done.3
  65.1 0.0 copy-done.4
  65.1 6.2 %first_conv.1 = (f32[18,10,16,128]{3,2,1,0:T(8,128)S(1)}, bf16[18,5,16,128]{3,2,1,0:T(8,128)(2,1)}, f32[2,128]{1,0:T(2,128)S(1)}) custom-call(bf16[4,16,32,128]{3,2,1,0:T(8,128)(2,1)S(1)} %copy-done.1, bf16[2,16,32,128]{3,2,1,0:T(8,128)(2,1)S(1)} %collective-permute-done.before_ref, bf16[6,2,32,128]{3,2,1,0:T(8,128)(2,1)S(1)} %get-tuple-element.25.above_ref, ...), custom_call_target="tpu_custom_call" | custom-call | tf_op jit(solution)/shard_map/first_conv/pallas_call | solution.py:305
  71.3 1.9 %collective-permute-start.5 = (bf16[18,5,16,128]{3,2,1,0:T(8,128)(2,1)}, bf16[18,5,16,128]{3,2,1,0:T(8,128)(2,1)S(1)}, u32[]{:S(2)}, u32[]{:S(2)}) collective-permute-start(bf16[18,5,16,128]{3,2,1,0:T(8,128)(2,1)} %get-tuple-element.31), channel_id=1, source_target_pairs={{0,128},{128,256},{256,384},{1,129},{129,257},{257,385},{2,130},{1... | collective-permute-start | bytes 1105928 | tf_op jit(solution)/shard_map/ppermute | solution.py:28
  73.2 11.2 %all-gather.12 = f32[8,2,128]{2,1,0:T(2,128)S(1)} all-gather(f32[1,2,128]{2,1,0:T(2,128)S(1)} %bitcast.25), channel_id=6, replica_groups=mesh['section'=4,'th_0'=4,'th_1'=4,'tw_0'=4,'tw_1'=2] {'tw_0','tw_1'}, dimensions={0}, use_global_device_ids=true | all-gather | bytes 9216 | tf_op jit(solution)/shard_map/all_gather | solution.py:22
  84.4 7.0 %all-gather.13 = f32[4,2,128]{2,1,0:T(2,128)S(1)} all-gather(f32[1,2,128]{2,1,0:T(2,128)S(1)} %bitcast.37), channel_id=7, replica_groups=mesh['section'=4,'th_0'=4,'th_1'=4,'tw_0'=4,'tw_1'=2] {'th_1'}, dimensions={0}, use_global_device_ids=true | all-gather | bytes 5120 | tf_op jit(solution)/shard_map/all_gather | solution.py:22
  91.4 9.6 %all-gather.14 = f32[4,2,128]{2,1,0:T(2,128)S(1)} all-gather(f32[1,2,128]{2,1,0:T(2,128)S(1)} %bitcast.41), channel_id=8, replica_groups=mesh['section'=4,'th_0'=4,'th_1'=4,'tw_0'=4,'tw_1'=2] {'section'}, dimensions={0}, use_global_device_ids=true | all-gather | bytes 5120 | tf_op jit(solution)/shard_map/all_gather | solution.py:22
  101.0 10.9 %all-gather.15.sums_ref = f32[4,2,128]{2,1,0:T(2,128)S(1)} all-gather(f32[1,2,128]{2,1,0:T(2,128)S(1)} %bitcast.39), channel_id=9, replica_groups=mesh['section'=4,'th_0'=4,'th_1'=4,'tw_0'=4,'tw_1'=2] {'th_0'}, dimensions={0}, use_global_device_ids=true | all-gather | bytes 5120 | tf_op jit(solution)/shard_map/all_gather | solution.py:331
  111.9 0.0 collective-permute-done.5.halo_ref
  111.9 0.0 copy-done.2
  111.9 5.1 %second_conv.1 = bf16[4,16,32,128]{3,2,1,0:T(8,128)(2,1)} custom-call(f32[18,10,16,128]{3,2,1,0:T(8,128)S(1)} %get-tuple-element.30.hidden_ref, bf16[18,5,16,128]{3,2,1,0:T(8,128)(2,1)S(1)} %collective-permute-done.5.halo_ref, f32[4,2,128]{2,1,0:T(2,128)S(1)} %all-gather.15.sums_ref, f32[1,128]{1,0:T(1,128)S(1)} %bitcast.28, f32[1,128]{1,0:T(1,128)S(1)} %bitcast.29, ...), custom_call_target="tpu_custom_call" | custom-call | tf_op jit(solution)/shard_map/second_conv/pallas_call | solution.py:333
  (19 shorter events, 0.2 us)
Async XLA Ops:
  0.0 1.0 copy-start
  1.0 64.0 %copy-start.1 = (bf16[4,16,32,128]{3,2,1,0:T(8,128)(2,1)S(1)}, bf16[4,16,32,128]{3,2,1,0:T(8,128)(2,1)}, u32[]{:S(2)}) copy-start(bf16[4,16,32,128]{3,2,1,0:T(8,128)(2,1)} %feat_ref.5) | copy-start | bytes 1572868
  1.0 64.0 %copy-start.3 = (f32[128]{0:T(128)S(1)}, f32[128]{0:T(128)}, u32[]{:S(2)}) copy-start(f32[128]{0:T(128)} %param.8) | copy-start | bytes 1540
  1.0 64.0 %copy-start.4 = (f32[128]{0:T(128)S(1)}, f32[128]{0:T(128)}, u32[]{:S(2)}) copy-start(f32[128]{0:T(128)} %param.9) | copy-start | bytes 1540
  1.3 14.4 %collective-permute-start = (bf16[2,16,32,128]{3,2,1,0:T(8,128)(2,1)S(1)}, bf16[2,16,32,128]{3,2,1,0:T(8,128)(2,1)S(1)}, u32[]{:S(2)}, u32[]{:S(2)}) collective-permute-start(bf16[2,16,32,128]{3,2,1,0:T(8,128)(2,1)S(1)} %get-tuple-element.19), channel_id=1, source_target_pairs={{0,128},{128,256},{256,384},{1,129},{129,257},{257,385},{2,130},{1... | collective-permute-start | bytes 786440 | tf_op jit(solution)/shard_map/ppermute | solution.py:28
  15.8 29.3 %collective-permute-start.2 = (bf16[6,2,32,128]{3,2,1,0:T(8,128)(2,1)S(1)}, bf16[6,2,32,128]{3,2,1,0:T(8,128)(2,1)S(1)}, u32[]{:S(2)}, u32[]{:S(2)}) collective-permute-start(bf16[6,2,32,128]{3,2,1,0:T(8,128)(2,1)S(1)} %get-tuple-element.42), channel_id=1, source_target_pairs={{8,16},{24,32},{40,48},{56,64},{72,80},{88,96},{104,112},{16,8},{3... | collective-permute-start | bytes 294920 | tf_op jit(solution)/shard_map/ppermute | solution.py:36
  16.4 28.7 %collective-permute-start.1 = (bf16[6,2,32,128]{3,2,1,0:T(8,128)(2,1)S(1)}, bf16[6,2,32,128]{3,2,1,0:T(8,128)(2,1)S(1)}, u32[]{:S(2)}, u32[]{:S(2)}) collective-permute-start(bf16[6,2,32,128]{3,2,1,0:T(8,128)(2,1)S(1)} %get-tuple-element.43), channel_id=1, source_target_pairs={{0,8},{16,24},{32,40},{48,56},{64,72},{80,88},{96,104},{112,120},{... | collective-permute-start | bytes 294920 | tf_op jit(solution)/shard_map/ppermute | solution.py:36
  45.1 66.8 %copy-start.2 = (bf16[3,3,3,128,128]{4,3,2,1,0:T(8,128)(2,1)S(1)}, bf16[3,3,3,128,128]{4,3,2,1,0:T(8,128)(2,1)}, u32[]{:S(2)}) copy-start(bf16[3,3,3,128,128]{4,3,2,1,0:T(8,128)(2,1)} %param.13) | copy-start | bytes 2654212
  45.1 66.8 %copy-start.5 = (f32[128]{0:T(128)S(1)}, f32[128]{0:T(128)}, u32[]{:S(2)}) copy-start(f32[128]{0:T(128)} %param.11) | copy-start | bytes 1540
  45.1 66.8 %copy-start.6 = (f32[128]{0:T(128)S(1)}, f32[128]{0:T(128)}, u32[]{:S(2)}) copy-start(f32[128]{0:T(128)} %param.12) | copy-start | bytes 1540
  45.4 19.6 %collective-permute-start.3 = (bf16[6,20,2,128]{3,2,1,0:T(2,128)(2,1)S(1)}, bf16[6,20,2,128]{3,2,1,0:T(2,128)(2,1)S(1)}, u32[]{:S(2)}, u32[]{:S(2)}) collective-permute-start(bf16[6,20,2,128]{3,2,1,0:T(2,128)(2,1)S(1)} %bitcast.33), channel_id=1, source_target_pairs={{0,1},{2,3},{4,5},{6,7},{1,0},{3,2},{5,4},{7,6},{8,9},{10,11},{12,... | collective-permute-start | bytes 184328 | tf_op jit(solution)/shard_map/ppermute | solution.py:36
  47.4 17.6 %collective-permute-start.4 = (bf16[6,20,2,128]{3,2,1,0:T(2,128)(2,1)S(1)}, bf16[6,20,2,128]{3,2,1,0:T(2,128)(2,1)S(1)}, u32[]{:S(2)}, u32[]{:S(2)}) collective-permute-start(bf16[6,20,2,128]{3,2,1,0:T(2,128)(2,1)S(1)} %get-tuple-element.33), channel_id=1, source_target_pairs={{1,2},{3,4},{5,6},{2,1},{4,3},{6,5},{9,10},{11,12},{13,14},{10,9},... | collective-permute-start | bytes 184328 | tf_op jit(solution)/shard_map/ppermute | solution.py:36
  71.3 40.7 %collective-permute-start.5 = (bf16[18,5,16,128]{3,2,1,0:T(8,128)(2,1)}, bf16[18,5,16,128]{3,2,1,0:T(8,128)(2,1)S(1)}, u32[]{:S(2)}, u32[]{:S(2)}) collective-permute-start(bf16[18,5,16,128]{3,2,1,0:T(8,128)(2,1)} %get-tuple-element.31), channel_id=1, source_target_pairs={{0,128},{128,256},{256,384},{1,129},{129,257},{257,385},{2,130},{1... | collective-permute-start | bytes 1105928 | tf_op jit(solution)/shard_map/ppermute | solution.py:28

commit v5 on v4

--- a/solution.py
+++ b/solution.py
@@ -175,7 +175,7 @@
             store_act(act_ref, h, m, pairs, row_ok, before_ok, column_ok)
         return 0
 
-    lax.fori_loop(0, ROWS1 + 2, fill, 0)
+    lax.fori_loop(0, ROWS1 + 2, fill, 0, unroll=2)
 
     clear_last_column(act_ref, ROWS1 + 2, COLS1 + 2)
     fetch.wait()
@@ -197,7 +197,7 @@
         return carry[0] + jnp.sum(own, 0), carry[1] + jnp.sum(own * own, 0)
 
     zero = jnp.zeros((8, 128), F32)
-    first, second = lax.fori_loop(1, ROWS1 - 1, total, (zero, zero))
+    first, second = lax.fori_loop(1, ROWS1 - 1, total, (zero, zero), unroll=4)
     out_sums_ref[0:1, :] = jnp.sum(first, 0, keepdims=True)
     out_sums_ref[1:2, :] = jnp.sum(second, 0, keepdims=True)
 
@@ -207,7 +207,7 @@
             halo_ref[h, j] = jnp.concatenate(both, 0).astype(BF16)
         return 0
 
-    lax.fori_loop(0, ROWS1, last_frames, 0)
+    lax.fori_loop(0, ROWS1, last_frames, 0, unroll=3)
 
 
 def second_body(count, hidden_ref, halo_ref, sums_ref, gain_ref, shift_ref, kernel_ref, feat_ref,
@@ -226,7 +226,7 @@
             store_act(act_ref, h, m, pairs, row_ok, before_ok, column_ok)
         return 0
 
-    lax.fori_loop(0, ROWS2 + 2, fill, 0)
+    lax.fori_loop(0, ROWS2 + 2, fill, 0, unroll=2)
 
     clear_last_column(act_ref, ROWS2 + 2, COLS2 + 2)
 
@@ -249,7 +249,7 @@
                 out_ref[t, h] = total.astype(BF16)
             return 0
 
-        lax.fori_loop(0, BLOCK2, spread, 0)
+        lax.fori_loop(0, BLOCK2, spread, 0, unroll=2)
         return 0
 
     lax.fori_loop(0, ROWS2 // BLOCK2, conv, 0)

time: 117 us -> 117 us (level)
  no operation moved by 1% of the time
where the time goes in v5:
time: 117 us; the launch traced here: 116 us
  blocking collectives  88.5 us (76%)
  starting transfers between devices  15.3 us (13%)
  Pallas kernels  11 us (9%)
    all_gather x6, blocking collectives, gathered_sum(): return jnp.sum(lax.all_gather(value, axis), axis=0)  60.6 us
    all_gather x2, blocking collectives, shards(): sums = lax.all_gather(sums, 'th_0')  27.9 us
    ppermute x4, starting transfers between devices, swap(): return lax.ppermute(value, axis, pairs + [(b, a) for a, b in pairs])  9.55 us
    pallas_call x1, Pallas kernels, shards(): pl.pallas_call(functools.partial(first_body, count), out_shape=(jax.Shape...  5.83 us
    ppermute x2, starting transfers between devices, shifted(): return lax.ppermute(value, axis, pairs)  5.74 us
    pallas_call x1, Pallas kernels, shards(): pl.pallas_call(functools.partial(second_body, count), out_shape=jax.Shape...  4.89 us
  transfers between devices with their start and end apart: 6, of which 0 were waited for; matrix products, arithmetic and copies ran while one was open for 0% of the time, Pallas kernels for 0%

profile of v5, /device:TPU:32, one launch (start us, length us, event | category | flops | bytes accessed | tf_op | source)
XLA Modules:
  0.0 116.5 jit_solution(270004777001260401)
XLA Ops:
  0.0 1.0 copy-done
  1.0 0.2 prepare.1
  1.3 3.8 %collective-permute-start = (bf16[2,16,32,128]{3,2,1,0:T(8,128)(2,1)S(1)}, bf16[2,16,32,128]{3,2,1,0:T(8,128)(2,1)S(1)}, u32[]{:S(2)}, u32[]{:S(2)}) collective-permute-start(bf16[2,16,32,128]{3,2,1,0:T(8,128)(2,1)S(1)} %get-tuple-element.19), channel_id=1, source_target_pairs={{0,128},{128,256},{256,384},{1,129},{129,257},{257,385},{2,130},{1... | collective-permute-start | bytes 786440 | tf_op jit(solution)/shard_map/ppermute | solution.py:28
  5.1 10.6 %all-gather.8 = f32[8,2,128]{2,1,0:T(2,128)S(1)} all-gather(f32[1,2,128]{2,1,0:T(2,128)S(1)} %bitcast.24), channel_id=2, replica_groups=mesh['section'=4,'th_0'=4,'th_1'=4,'tw_0'=4,'tw_1'=2] {'tw_0','tw_1'}, dimensions={0}, use_global_device_ids=true | all-gather | bytes 9216 | tf_op jit(solution)/shard_map/all_gather | solution.py:22
  15.7 0.0 collective-permute-done.before_ref
  15.8 0.7 collective-permute-start.2
  16.4 6.3 %collective-permute-start.1 = (bf16[6,2,32,128]{3,2,1,0:T(8,128)(2,1)S(1)}, bf16[6,2,32,128]{3,2,1,0:T(8,128)(2,1)S(1)}, u32[]{:S(2)}, u32[]{:S(2)}) collective-permute-start(bf16[6,2,32,128]{3,2,1,0:T(8,128)(2,1)S(1)} %get-tuple-element.43), channel_id=1, source_target_pairs={{0,8},{16,24},{32,40},{48,56},{64,72},{80,88},{96,104},{112,120},{... | collective-permute-start | bytes 294920 | tf_op jit(solution)/shard_map/ppermute | solution.py:36
  22.8 13.8 %all-gather.9 = f32[4,2,128]{2,1,0:T(2,128)S(1)} all-gather(f32[1,2,128]{2,1,0:T(2,128)S(1)} %bitcast.36), channel_id=3, replica_groups=mesh['section'=4,'th_0'=4,'th_1'=4,'tw_0'=4,'tw_1'=2] {'th_1'}, dimensions={0}, use_global_device_ids=true | all-gather | bytes 5120 | tf_op jit(solution)/shard_map/all_gather | solution.py:22
  36.6 8.5 %all-gather.10 = f32[4,2,128]{2,1,0:T(2,128)S(1)} all-gather(f32[1,2,128]{2,1,0:T(2,128)S(1)} %bitcast.40), channel_id=4, replica_groups=mesh['section'=4,'th_0'=4,'th_1'=4,'tw_0'=4,'tw_1'=2] {'section'}, dimensions={0}, use_global_device_ids=true | all-gather | bytes 5120 | tf_op jit(solution)/shard_map/all_gather | solution.py:22
  45.1 0.0 collective-permute-done.2
  45.1 0.0 collective-permute-done.1
  45.1 0.0 copy-start.2
  45.1 0.0 copy-start.5
  45.1 0.0 copy-start.6
  45.2 0.2 broadcast_select_fusion.2
  45.4 1.9 %collective-permute-start.3 = (bf16[6,20,2,128]{3,2,1,0:T(2,128)(2,1)S(1)}, bf16[6,20,2,128]{3,2,1,0:T(2,128)(2,1)S(1)}, u32[]{:S(2)}, u32[]{:S(2)}) collective-permute-start(bf16[6,20,2,128]{3,2,1,0:T(2,128)(2,1)S(1)} %bitcast.33), channel_id=1, source_target_pairs={{0,1},{2,3},{4,5},{6,7},{1,0},{3,2},{5,4},{7,6},{8,9},{10,11},{12,... | collective-permute-start | bytes 184328 | tf_op jit(solution)/shard_map/ppermute | solution.py:36
  47.4 0.7 collective-permute-start.4
  48.0 17.0 %all-gather.11.sums_ref = f32[4,2,128]{2,1,0:T(2,128)S(1)} all-gather(f32[1,2,128]{2,1,0:T(2,128)S(1)} %bitcast.38), channel_id=5, replica_groups=mesh['section'=4,'th_0'=4,'th_1'=4,'tw_0'=4,'tw_1'=2] {'th_0'}, dimensions={0}, use_global_device_ids=true | all-gather | bytes 5120 | tf_op jit(solution)/shard_map/all_gather | solution.py:303
  65.0 0.0 collective-permute-done.3
  65.0 0.0 collective-permute-done.4
  65.0 0.0 copy-done.1
  65.1 0.0 copy-done.3
  65.1 0.0 copy-done.4
  65.1 5.8 %first_conv.1 = (f32[18,10,16,128]{3,2,1,0:T(8,128)S(1)}, bf16[18,5,16,128]{3,2,1,0:T(8,128)(2,1)}, f32[2,128]{1,0:T(2,128)S(1)}) custom-call(bf16[4,16,32,128]{3,2,1,0:T(8,128)(2,1)S(1)} %copy-done.1, bf16[2,16,32,128]{3,2,1,0:T(8,128)(2,1)S(1)} %collective-permute-done.before_ref, bf16[6,2,32,128]{3,2,1,0:T(8,128)(2,1)S(1)} %get-tuple-element.25.above_ref, ...), custom_call_target="tpu_custom_call" | custom-call | tf_op jit(solution)/shard_map/first_conv/pallas_call | solution.py:305
  70.9 1.9 %collective-permute-start.5 = (bf16[18,5,16,128]{3,2,1,0:T(8,128)(2,1)}, bf16[18,5,16,128]{3,2,1,0:T(8,128)(2,1)S(1)}, u32[]{:S(2)}, u32[]{:S(2)}) collective-permute-start(bf16[18,5,16,128]{3,2,1,0:T(8,128)(2,1)} %get-tuple-element.31), channel_id=1, source_target_pairs={{0,128},{128,256},{256,384},{1,129},{129,257},{257,385},{2,130},{1... | collective-permute-start | bytes 1105928 | tf_op jit(solution)/shard_map/ppermute | solution.py:28
  72.8 11.2 %all-gather.12 = f32[8,2,128]{2,1,0:T(2,128)S(1)} all-gather(f32[1,2,128]{2,1,0:T(2,128)S(1)} %bitcast.25), channel_id=6, replica_groups=mesh['section'=4,'th_0'=4,'th_1'=4,'tw_0'=4,'tw_1'=2] {'tw_0','tw_1'}, dimensions={0}, use_global_device_ids=true | all-gather | bytes 9216 | tf_op jit(solution)/shard_map/all_gather | solution.py:22
  84.0 7.0 %all-gather.13 = f32[4,2,128]{2,1,0:T(2,128)S(1)} all-gather(f32[1,2,128]{2,1,0:T(2,128)S(1)} %bitcast.37), channel_id=7, replica_groups=mesh['section'=4,'th_0'=4,'th_1'=4,'tw_0'=4,'tw_1'=2] {'th_1'}, dimensions={0}, use_global_device_ids=true | all-gather | bytes 5120 | tf_op jit(solution)/shard_map/all_gather | solution.py:22
  91.0 9.6 %all-gather.14 = f32[4,2,128]{2,1,0:T(2,128)S(1)} all-gather(f32[1,2,128]{2,1,0:T(2,128)S(1)} %bitcast.41), channel_id=8, replica_groups=mesh['section'=4,'th_0'=4,'th_1'=4,'tw_0'=4,'tw_1'=2] {'section'}, dimensions={0}, use_global_device_ids=true | all-gather | bytes 5120 | tf_op jit(solution)/shard_map/all_gather | solution.py:22
  100.6 10.9 %all-gather.15.sums_ref = f32[4,2,128]{2,1,0:T(2,128)S(1)} all-gather(f32[1,2,128]{2,1,0:T(2,128)S(1)} %bitcast.39), channel_id=9, replica_groups=mesh['section'=4,'th_0'=4,'th_1'=4,'tw_0'=4,'tw_1'=2] {'th_0'}, dimensions={0}, use_global_device_ids=true | all-gather | bytes 5120 | tf_op jit(solution)/shard_map/all_gather | solution.py:331
  111.6 0.0 collective-permute-done.5.halo_ref
  111.6 0.0 copy-done.5
  111.6 4.9 %second_conv.1 = bf16[4,16,32,128]{3,2,1,0:T(8,128)(2,1)} custom-call(f32[18,10,16,128]{3,2,1,0:T(8,128)S(1)} %get-tuple-element.30.hidden_ref, bf16[18,5,16,128]{3,2,1,0:T(8,128)(2,1)S(1)} %collective-permute-done.5.halo_ref, f32[4,2,128]{2,1,0:T(2,128)S(1)} %all-gather.15.sums_ref, f32[1,128]{1,0:T(1,128)S(1)} %bitcast.28, f32[1,128]{1,0:T(1,128)S(1)} %bitcast.29, ...), custom_call_target="tpu_custom_call" | custom-call | tf_op jit(solution)/shard_map/second_conv/pallas_call | solution.py:333
  (19 shorter events, 0.2 us)
Async XLA Ops:
  0.0 1.0 copy-start
  1.0 64.0 %copy-start.1 = (bf16[4,16,32,128]{3,2,1,0:T(8,128)(2,1)S(1)}, bf16[4,16,32,128]{3,2,1,0:T(8,128)(2,1)}, u32[]{:S(2)}) copy-start(bf16[4,16,32,128]{3,2,1,0:T(8,128)(2,1)} %feat_ref.5) | copy-start | bytes 1572868
  1.0 64.0 %copy-start.3 = (f32[128]{0:T(128)S(1)}, f32[128]{0:T(128)}, u32[]{:S(2)}) copy-start(f32[128]{0:T(128)} %param.8) | copy-start | bytes 1540
  1.0 64.0 %copy-start.4 = (f32[128]{0:T(128)S(1)}, f32[128]{0:T(128)}, u32[]{:S(2)}) copy-start(f32[128]{0:T(128)} %param.9) | copy-start | bytes 1540
  1.3 14.4 %collective-permute-start = (bf16[2,16,32,128]{3,2,1,0:T(8,128)(2,1)S(1)}, bf16[2,16,32,128]{3,2,1,0:T(8,128)(2,1)S(1)}, u32[]{:S(2)}, u32[]{:S(2)}) collective-permute-start(bf16[2,16,32,128]{3,2,1,0:T(8,128)(2,1)S(1)} %get-tuple-element.19), channel_id=1, source_target_pairs={{0,128},{128,256},{256,384},{1,129},{129,257},{257,385},{2,130},{1... | collective-permute-start | bytes 786440 | tf_op jit(solution)/shard_map/ppermute | solution.py:28
  15.8 29.3 %collective-permute-start.2 = (bf16[6,2,32,128]{3,2,1,0:T(8,128)(2,1)S(1)}, bf16[6,2,32,128]{3,2,1,0:T(8,128)(2,1)S(1)}, u32[]{:S(2)}, u32[]{:S(2)}) collective-permute-start(bf16[6,2,32,128]{3,2,1,0:T(8,128)(2,1)S(1)} %get-tuple-element.42), channel_id=1, source_target_pairs={{8,16},{24,32},{40,48},{56,64},{72,80},{88,96},{104,112},{16,8},{3... | collective-permute-start | bytes 294920 | tf_op jit(solution)/shard_map/ppermute | solution.py:36
  16.4 28.7 %collective-permute-start.1 = (bf16[6,2,32,128]{3,2,1,0:T(8,128)(2,1)S(1)}, bf16[6,2,32,128]{3,2,1,0:T(8,128)(2,1)S(1)}, u32[]{:S(2)}, u32[]{:S(2)}) collective-permute-start(bf16[6,2,32,128]{3,2,1,0:T(8,128)(2,1)S(1)} %get-tuple-element.43), channel_id=1, source_target_pairs={{0,8},{16,24},{32,40},{48,56},{64,72},{80,88},{96,104},{112,120},{... | collective-permute-start | bytes 294920 | tf_op jit(solution)/shard_map/ppermute | solution.py:36
  45.1 66.5 %copy-start.2 = (bf16[3,3,3,128,128]{4,3,2,1,0:T(8,128)(2,1)S(1)}, bf16[3,3,3,128,128]{4,3,2,1,0:T(8,128)(2,1)}, u32[]{:S(2)}) copy-start(bf16[3,3,3,128,128]{4,3,2,1,0:T(8,128)(2,1)} %param.13) | copy-start | bytes 2654212
  45.1 66.5 %copy-start.5 = (f32[128]{0:T(128)S(1)}, f32[128]{0:T(128)}, u32[]{:S(2)}) copy-start(f32[128]{0:T(128)} %param.11) | copy-start | bytes 1540
  45.1 66.5 %copy-start.6 = (f32[128]{0:T(128)S(1)}, f32[128]{0:T(128)}, u32[]{:S(2)}) copy-start(f32[128]{0:T(128)} %param.12) | copy-start | bytes 1540
  45.4 19.6 %collective-permute-start.3 = (bf16[6,20,2,128]{3,2,1,0:T(2,128)(2,1)S(1)}, bf16[6,20,2,128]{3,2,1,0:T(2,128)(2,1)S(1)}, u32[]{:S(2)}, u32[]{:S(2)}) collective-permute-start(bf16[6,20,2,128]{3,2,1,0:T(2,128)(2,1)S(1)} %bitcast.33), channel_id=1, source_target_pairs={{0,1},{2,3},{4,5},{6,7},{1,0},{3,2},{5,4},{7,6},{8,9},{10,11},{12,... | collective-permute-start | bytes 184328 | tf_op jit(solution)/shard_map/ppermute | solution.py:36
  47.4 17.6 %collective-permute-start.4 = (bf16[6,20,2,128]{3,2,1,0:T(2,128)(2,1)S(1)}, bf16[6,20,2,128]{3,2,1,0:T(2,128)(2,1)S(1)}, u32[]{:S(2)}, u32[]{:S(2)}) collective-permute-start(bf16[6,20,2,128]{3,2,1,0:T(2,128)(2,1)S(1)} %get-tuple-element.33), channel_id=1, source_target_pairs={{1,2},{3,4},{5,6},{2,1},{4,3},{6,5},{9,10},{11,12},{13,14},{10,9},... | collective-permute-start | bytes 184328 | tf_op jit(solution)/shard_map/ppermute | solution.py:36
  70.9 40.7 %collective-permute-start.5 = (bf16[18,5,16,128]{3,2,1,0:T(8,128)(2,1)}, bf16[18,5,16,128]{3,2,1,0:T(8,128)(2,1)S(1)}, u32[]{:S(2)}, u32[]{:S(2)}) collective-permute-start(bf16[18,5,16,128]{3,2,1,0:T(8,128)(2,1)} %get-tuple-element.31), channel_id=1, source_target_pairs={{0,128},{128,256},{256,384},{1,129},{129,257},{257,385},{2,130},{1... | collective-permute-start | bytes 1105928 | tf_op jit(solution)/shard_map/ppermute | solution.py:28
